TPU v7x, 32 devices: a whole 2x2x4 slice. The times are simulated.
32 devices in a mesh: dp: 4 (over z), row: 2 (over y), col: 4 (over x, core).
Axes of the slice: x: 2, y: 2, z: 4, core: 2. Of those that a mesh axis runs over, the one named last changes fastest.
Arguments:
- block_input: bfloat16 [18816, 512], P(('dp', 'row')), may hold values from -6 to 6
- cotangent: bfloat16 [18816, 512], P(('dp', 'row')), may hold values from -6 to 6
- region_ids: int32 [196], replicated, may hold values from 0 to 3
- rel_index: int32 [49, 49], replicated, may hold values from 0 to 168
- first_gain: float32 [2, 512], replicated, may hold values from 0.5 to 1.5
- first_offset: float32 [2, 512], replicated, may hold values from -3 to 3
- triple_weight: bfloat16 [2, 512, 3, 512], P(None, 'row', None, 'col'), may hold values from -0.25 to 0.25
- triple_bias: float32 [2, 3, 512], P(None, None, 'col'), may hold values from -3 to 3
- rel_table: float32 [2, 169, 16], P(None, None, 'col'), may hold values from -4 to 4
- project_weight: bfloat16 [2, 512, 512], P(None, 'row', 'col'), may hold values from -0.375 to 0.375
- project_bias: float32 [2, 512], replicated, may hold values from -3 to 3
- second_gain: float32 [2, 512], replicated, may hold values from 0.5 to 1.5
- second_offset: float32 [2, 512], replicated, may hold values from -3 to 3
- expand_weight: bfloat16 [2, 512, 2048], P(None, 'row', 'col'), may hold values from -0.25 to 0.25
- expand_bias: float32 [2, 2048], P(None, 'col'), may hold values from -3 to 3
- reduce_weight: bfloat16 [2, 512, 2048], P(None, 'row', 'col'), may hold values from -0.125 to 0.125
- reduce_bias: float32 [2, 512], replicated, may hold values from -3 to 3
Outputs:
- block_output: float32 [18816, 512], P(('dp', 'row'))
- input_grad: float32 [18816, 512], P(('dp', 'row'))
- first_gain_grad: float32 [2, 512], replicated
- first_offset_grad: float32 [2, 512], replicated
- triple_weight_grad: float32 [2, 512, 3, 512], P(None, 'row', None, 'col')
- triple_bias_grad: float32 [2, 3, 512], P(None, None, 'col')
- rel_table_grad: float32 [2, 169, 16], P(None, None, 'col')
- project_weight_grad: float32 [2, 512, 512], P(None, 'row', 'col')
- project_bias_grad: float32 [2, 512], replicated
- second_gain_grad: float32 [2, 512], replicated
- second_offset_grad: float32 [2, 512], replicated
- expand_weight_grad: float32 [2, 512, 2048], P(None, 'row', 'col')
- expand_bias_grad: float32 [2, 2048], P(None, 'col')
- reduce_weight_grad: float32 [2, 512, 2048], P(None, 'row', 'col')
- reduce_bias_grad: float32 [2, 512], replicated
Inputs may be any that keep to these rules, and one draw needn't show every extreme that they name: region_ids[p] is the region of position p of the rolled 14 x 14 grid, row-major. rel_index[i, j] selects the row of rel_table for query position i and key position j of a window, both row-major.
All inputs are finite; a program needn't handle non-finite values.
Results may differ from a plain program's by a relative error of at most 0.038.
Values may be sent and summed in bfloat16 or wider, within the bound.
A program may use at most 192 MiB of HBM per device.

v0:
```python
import math

import jax
import jax.numpy as jnp
from jax import lax
from jax.sharding import PartitionSpec as P

LAYERS = 2
SIDE = 14
WIN = 7
SHIFT = 3
IMG_BLOCK = 3
HEAD = 32
RELS = 169


EPSILON = 1e-05
MASKED = -100.0
HIGHEST = lax.Precision.HIGHEST


def layer_norm(hidden, scales, offsets):
    average = jnp.mean(hidden, axis=-1, keepdims=True)
    centered = hidden - average
    variance = jnp.mean(centered * centered, axis=-1, keepdims=True)
    inverse = lax.rsqrt(variance + EPSILON)
    normed = centered * inverse
    return (normed * scales + offsets, normed, inverse)


def norm_backward(upstream, normed, inverse, scales):
    weighted = upstream * scales
    first_mean = jnp.mean(weighted, axis=-1, keepdims=True)
    second_mean = jnp.mean(weighted * normed, axis=-1, keepdims=True)
    result = inverse * (weighted - first_mean - normed * second_mean)
    return (result, jnp.sum(upstream * normed, axis=0), jnp.sum(upstream, axis=0))


def gelu_exact(values):
    return jax.nn.gelu(values, approximate=False)


def to_windows(tokens, images, offset):
    blocks = SIDE // WIN
    columns = tokens.shape[-1]
    spatial = tokens.reshape(images, SIDE, SIDE, columns)
    if offset:
        spatial = jnp.roll(spatial, (-offset, -offset), axis=(1, 2))
    spatial = spatial.reshape(images, blocks, WIN, blocks, WIN, columns).transpose(0, 1, 3, 2, 4, 5)
    return spatial.reshape(images * blocks * blocks, WIN * WIN, columns)


def from_windows(windows, images, offset):
    blocks = SIDE // WIN
    columns = windows.shape[-1]
    spatial = windows.reshape(images, blocks, blocks, WIN, WIN, columns).transpose(0, 1, 3, 2, 4, 5)
    spatial = spatial.reshape(images, SIDE, SIDE, columns)
    if offset:
        spatial = jnp.roll(spatial, (offset, offset), axis=(1, 2))
    return spatial.reshape(images * SIDE * SIDE, columns)


def region_mask(region_ids):
    cells = to_windows(region_ids.reshape(SIDE * SIDE, 1), 1, 0)[:, :, 0]
    return jnp.where(cells[:, :, None] == cells[:, None, :], 0.0, MASKED).astype(jnp.float32)


def rel_onehot(rel_index):
    return (rel_index.reshape(-1)[:, None] == jnp.arange(RELS, dtype=jnp.int32)[None, :]).astype(
        jnp.float32
    )


def rel_bias(onehot, table):
    count = table.shape[1]
    return jnp.dot(onehot, table, precision=HIGHEST).T.reshape(count, WIN * WIN, WIN * WIN)


def window_scores(query_win, key_win, bias, layer_mask, images):
    scores = jnp.einsum("wihd,wjhd->whij", query_win, key_win, preferred_element_type=jnp.float32)
    scores = scores + bias[None]
    if layer_mask is not None:
        shaped = scores.reshape((images, layer_mask.shape[0]) + scores.shape[1:])
        scores = (shaped + layer_mask[None, :, None]).reshape(scores.shape)
    return scores


def attend_forward(query_win, key_win, value_win, bias, layer_mask, images):
    scores = window_scores(query_win, key_win, bias, layer_mask, images)
    log_total = jnp.log(jnp.sum(jnp.exp(scores), axis=-1))
    probs = jnp.exp(scores - log_total[..., None]).astype(jnp.bfloat16)
    output = jnp.einsum("whij,wjhd->wihd", probs, value_win, preferred_element_type=jnp.float32)
    return (output.astype(jnp.bfloat16), log_total)


def attend_backward(
    query_win, key_win, value_win, output, log_total, out_grad, bias, layer_mask, images
):
    scores = window_scores(query_win, key_win, bias, layer_mask, images)
    probs = jnp.exp(scores - log_total[..., None])
    probs_low = probs.astype(jnp.bfloat16)
    value_grad = jnp.einsum(
        "whij,wihd->wjhd", probs_low, out_grad, preferred_element_type=jnp.float32
    )
    prob_grad = jnp.einsum(
        "wihd,wjhd->whij", out_grad, value_win, preferred_element_type=jnp.float32
    )
    delta = jnp.sum(out_grad.astype(jnp.float32) * output.astype(jnp.float32), axis=-1).transpose(
        0, 2, 1
    )
    score_grad = probs * (prob_grad - delta[..., None])
    bias_grad = jnp.sum(score_grad, axis=0)
    score_low = score_grad.astype(jnp.bfloat16)
    query_grad = jnp.einsum(
        "whij,wjhd->wihd", score_low, key_win, preferred_element_type=jnp.float32
    ) * HEAD ** (-0.5)
    key_grad = jnp.einsum(
        "whij,wihd->wjhd", score_low, query_win, preferred_element_type=jnp.float32
    )
    return (query_grad, key_grad, value_grad, bias_grad)


def shards(
    block_input,
    cotangent,
    region_ids,
    rel_index,
    first_gain,
    first_offset,
    triple_weight,
    triple_bias,
    rel_table,
    project_weight,
    project_bias,
    second_gain,
    second_offset,
    expand_weight,
    expand_bias,
    reduce_weight,
    reduce_bias,
):
    triple_full, project_full, expand_full, reduce_full = (
        lax.all_gather(triple_weight, "row", axis=1, tiled=True),
        lax.all_gather(project_weight, "row", axis=1, tiled=True),
        lax.all_gather(expand_weight, "row", axis=1, tiled=True),
        lax.all_gather(reduce_weight, "row", axis=1, tiled=True),
    )
    grad_scale = 1.0 / math.sqrt(block_input.shape[0] * lax.axis_size("dp") * lax.axis_size("row"))
    triple_bias_used, rel_table_used, expand_bias_used = (triple_bias, rel_table, expand_bias)
    rows_in, cot_in = (block_input, cotangent)

    def out_sum(left, weight):
        partial_value = jnp.einsum("tkc,ekc->te", left, weight, preferred_element_type=jnp.float32)
        return lax.psum(partial_value.astype(jnp.bfloat16), "col").astype(jnp.float32)

    def back_sum(left, weight):
        partial_value = jnp.einsum("tkc,ekc->te", left, weight, preferred_element_type=jnp.float32)
        return lax.psum(partial_value.astype(jnp.bfloat16), "col").astype(jnp.float32)

    tokens = rows_in.shape[0]
    images = tokens // (SIDE * SIDE)
    per_image = (SIDE // WIN) ** 2
    windows = images * per_image
    block_count = images // IMG_BLOCK
    local_heads = rel_table_used.shape[2]
    local_width = local_heads * HEAD
    onehot = rel_onehot(rel_index)
    shift_mask = region_mask(region_ids)
    scaling = jnp.array([HEAD ** (-0.5), 1.0, 1.0], dtype=jnp.float32)[:, None]
    hidden = rows_in.astype(jnp.float32)
    stored = []
    for layer_index in range(LAYERS):
        offset = SHIFT if layer_index % 2 == 1 else 0
        layer_mask = shift_mask if offset else None
        bias = rel_bias(onehot, rel_table_used[layer_index])
        normed, first_hat, first_inv = layer_norm(
            hidden, first_gain[layer_index], first_offset[layer_index]
        )
        first_low = normed.astype(jnp.bfloat16)
        triple = jnp.einsum(
            "td,dkc->tkc", first_low, triple_full[layer_index], preferred_element_type=jnp.float32
        )
        triple_low = ((triple + triple_bias_used[layer_index]) * scaling).astype(jnp.bfloat16)
        windowed = to_windows(triple_low.reshape(tokens, 3 * local_width), images, offset)
        windowed = windowed.reshape(
            block_count, IMG_BLOCK * per_image, WIN * WIN, 3, local_heads, HEAD
        )
        query_blk = windowed[:, :, :, 0]
        key_blk = windowed[:, :, :, 1]
        value_blk = windowed[:, :, :, 2]

        def forward_block(inputs, bias=bias, layer_mask=layer_mask):
            return attend_forward(inputs[0], inputs[1], inputs[2], bias, layer_mask, IMG_BLOCK)

        attn_out, log_total = lax.map(forward_block, (query_blk, key_blk, value_blk))
        merged = from_windows(attn_out.reshape(windows, WIN * WIN, local_width), images, offset)
        middle = (
            hidden
            + out_sum(merged[:, None], project_full[layer_index][:, None])
            + project_bias[layer_index]
        )
        normed, second_hat, second_inv = layer_norm(
            middle, second_gain[layer_index], second_offset[layer_index]
        )
        second_low = normed.astype(jnp.bfloat16)
        pre_act = (
            jnp.dot(second_low, expand_full[layer_index], preferred_element_type=jnp.float32)
            + expand_bias_used[layer_index]
        )
        act_low = gelu_exact(pre_act).astype(jnp.bfloat16)
        stored.append(
            (
                first_hat,
                first_inv,
                first_low,
                query_blk,
                key_blk,
                value_blk,
                attn_out,
                log_total,
                merged,
                second_hat,
                second_inv,
                second_low,
                pre_act,
                act_low,
                bias,
                layer_mask,
                offset,
            )
        )
        hidden = (
            middle
            + out_sum(act_low[:, None], reduce_full[layer_index][:, None])
            + reduce_bias[layer_index]
        )
    grad = cot_in.astype(jnp.float32)
    collected = [None] * LAYERS
    for layer_index in reversed(range(LAYERS)):
        (
            first_hat,
            first_inv,
            first_low,
            query_blk,
            key_blk,
            value_blk,
            attn_out,
            log_total,
            merged,
            second_hat,
            second_inv,
            second_low,
            pre_act,
            act_low,
            bias,
            layer_mask,
            offset,
        ) = stored[layer_index]
        reduce_bias_grad = jnp.sum(grad, axis=0)
        grad_low = grad.astype(jnp.bfloat16)
        reduce_weight_grad = jnp.einsum(
            "te,tc->ec", grad_low, act_low, preferred_element_type=jnp.float32
        )
        act_grad = jnp.einsum(
            "te,ec->tc", grad_low, reduce_full[layer_index], preferred_element_type=jnp.float32
        )
        pre_grad = jax.vjp(gelu_exact, pre_act)[1](act_grad)[0]
        expand_bias_grad = jnp.sum(pre_grad, axis=0)
        pre_low = pre_grad.astype(jnp.bfloat16)
        expand_weight_grad = jnp.einsum(
            "td,tc->dc", second_low, pre_low, preferred_element_type=jnp.float32
        )
        upstream = back_sum(pre_low[:, None], expand_full[layer_index][:, None])
        back, second_gain_grad, second_offset_grad = norm_backward(
            upstream, second_hat, second_inv, second_gain[layer_index]
        )
        grad = grad + back
        project_bias_grad = jnp.sum(grad, axis=0)
        grad_low = grad.astype(jnp.bfloat16)
        project_weight_grad = jnp.einsum(
            "te,tc->ec", grad_low, merged, preferred_element_type=jnp.float32
        )
        merged_grad = jnp.einsum(
            "te,ec->tc", grad_low, project_full[layer_index], preferred_element_type=jnp.float32
        ).astype(jnp.bfloat16)
        out_grad_blk = to_windows(merged_grad, images, offset).reshape(
            block_count, IMG_BLOCK * per_image, WIN * WIN, local_heads, HEAD
        )

        def backward_block(inputs, bias=bias, layer_mask=layer_mask):
            return attend_backward(
                inputs[0],
                inputs[1],
                inputs[2],
                inputs[3],
                inputs[4],
                inputs[5],
                bias,
                layer_mask,
                IMG_BLOCK,
            )

        query_grad, key_grad, value_grad, bias_grad = lax.map(
            backward_block, (query_blk, key_blk, value_blk, attn_out, log_total, out_grad_blk)
        )
        bias_total = jnp.sum(bias_grad, axis=0)
        rel_table_grad = jnp.dot(onehot.T, bias_total.reshape(local_heads, -1).T, precision=HIGHEST)
        stacked = jnp.stack((query_grad, key_grad, value_grad), axis=3).reshape(
            windows, WIN * WIN, 3 * local_width
        )
        triple_grad = from_windows(stacked, images, offset).reshape(tokens, 3, local_width)
        triple_bias_grad = jnp.sum(triple_grad, axis=0)
        triple_low_grad = triple_grad.astype(jnp.bfloat16)
        triple_weight_grad = jnp.einsum(
            "td,tkc->dkc", first_low, triple_low_grad, preferred_element_type=jnp.float32
        )
        upstream = back_sum(triple_low_grad, triple_full[layer_index])
        back, first_gain_grad, first_offset_grad = norm_backward(
            upstream, first_hat, first_inv, first_gain[layer_index]
        )
        grad = grad + back
        collected[layer_index] = (
            first_gain_grad,
            first_offset_grad,
            triple_weight_grad,
            triple_bias_grad,
            rel_table_grad,
            project_weight_grad,
            project_bias_grad,
            second_gain_grad,
            second_offset_grad,
            expand_weight_grad,
            expand_bias_grad,
            reduce_weight_grad,
            reduce_bias_grad,
        )
    stacked_grads = [
        jnp.stack([collected[index][slot] for index in range(LAYERS)]) * grad_scale
        for slot in range(13)
    ]
    summed = (
        lax.psum(stacked_grads[0].astype(jnp.bfloat16), ("dp", "row")).astype(jnp.float32),
        lax.psum(stacked_grads[1].astype(jnp.bfloat16), ("dp", "row")).astype(jnp.float32),
        lax.psum(stacked_grads[2].astype(jnp.bfloat16), ("dp", "row")).astype(jnp.float32),
        lax.psum(stacked_grads[3].astype(jnp.bfloat16), ("dp", "row")).astype(jnp.float32),
        lax.psum(stacked_grads[4].astype(jnp.bfloat16), ("dp", "row")).astype(jnp.float32),
        lax.psum(stacked_grads[5].astype(jnp.bfloat16), ("dp", "row")).astype(jnp.float32),
        lax.psum(stacked_grads[6].astype(jnp.bfloat16), ("dp", "row")).astype(jnp.float32),
        lax.psum(stacked_grads[7].astype(jnp.bfloat16), ("dp", "row")).astype(jnp.float32),
        lax.psum(stacked_grads[8].astype(jnp.bfloat16), ("dp", "row")).astype(jnp.float32),
        lax.psum(stacked_grads[9].astype(jnp.bfloat16), ("dp", "row")).astype(jnp.float32),
        lax.psum(stacked_grads[10].astype(jnp.bfloat16), ("dp", "row")).astype(jnp.float32),
        lax.psum(stacked_grads[11].astype(jnp.bfloat16), ("dp", "row")).astype(jnp.float32),
        lax.psum(stacked_grads[12].astype(jnp.bfloat16), ("dp", "row")).astype(jnp.float32),
    )
    row_width = triple_weight.shape[1]
    start = lax.axis_index("row") * row_width
    final = list(summed)
    for slot in (2, 5, 9, 11):
        final[slot] = lax.dynamic_slice_in_dim(summed[slot], start, row_width, 1)
    return (
        hidden,
        grad,
        final[0],
        final[1],
        final[2],
        final[3],
        final[4],
        final[5],
        final[6],
        final[7],
        final[8],
        final[9],
        final[10],
        final[11],
        final[12],
    )


def solution(mesh):
    placed = (
        P(("dp", "row"), None),
        P(("dp", "row"), None),
        P(),
        P(),
        P(),
        P(),
        P(None, "row", None, "col"),
        P(None, None, "col"),
        P(None, None, "col"),
        P(None, "row", "col"),
        P(),
        P(),
        P(),
        P(None, "row", "col"),
        P(None, "col"),
        P(None, "row", "col"),
        P(),
    )
    return jax.shard_map(
        shards,
        mesh=mesh,
        in_specs=placed,
        out_specs=(
            P(("dp", "row"), None),
            P(("dp", "row"), None),
            P(),
            P(),
            P(None, "row", None, "col"),
            P(None, None, "col"),
            P(None, None, "col"),
            P(None, "row", "col"),
            P(),
            P(),
            P(),
            P(None, "row", "col"),
            P(None, "col"),
            P(None, "row", "col"),
            P(),
        ),
        check_vma=False,
    )
```

profile of v0, /device:TPU:0, one launch (start us, length us, event | category | flops | bytes accessed | tf_op | source)
XLA Modules:
  0.0 1161.2 jit_solution(16982457570958544198)
XLA Ops:
  13.2 12.8 %all_gather.12 = bf16[2,512,3,128]{3,1,2,0:T(8,128)(2,1)S(1)} all-gather(bf16[2,256,3,128]{3,1,2,0:T(8,128)(2,1)S(1)} %copy-done.35), channel_id=1, replica_groups=mesh['dp'=4,'row'=2,'col'=4] {'row'}, dimensions={1}, use_global_device_ids=true | all-gather | bytes 1179648 | tf_op jit(solution)/shard_map/all_gather | solution.py:143
  28.4 10.2 copy.44
  48.8 11.4 reshape_reshape.30
  90.2 16.8 %while.58 = (s32[]{:T(128)}, bf16[4,12,49,4,32]{2,4,3,1,0:T(8,128)(2,1)}, f32[4,12,4,49]{3,2,1,0:T(4,128)S(1)}, bf16[4,12,49,4,32]{2,4,3,1,0:T(8,128)(2,1)}, bf1...) while((s32[]{:T(128)}, ...), condition=%wide.region_4.5_spmd, body=%wide.region_2.4_spmd.sunk | while | flops 15285650 | bytes 2775849 | solution.py:195
  130.4 56.9 %all-reduce.12.cloned.1.call-done = bf16[2352,512]{1,0:T(8,128)(2,1)} async-done(((bf16[2352,512]{1,0:T(8,128)(2,1)}), bf16[2352,512]{1,0:T(8,128)(2,1)}) %all-reduce.12.cloned.1.call-update) | async-done | bytes 2408464 | tf_op jit(solution)/shard_map/psum | solution.py:154
  194.4 14.7 %multiply_convert_fusion.1 = (bf16[2352,512]{1,0:T(8,128)(2,1)}, f32[2352,512]{1,0:T(8,128)}, f32[2352,512]{1,0:T(8,128)}) fusion(f32[512]{0:T(512)S(1)} %bitcast.503, bf16[2352,512]{1,0:T(8,128)(2,1)} %add_convert_fusion.2, bf16[2,512,512]{2,1,0:T(8,128)(2,1)} %all-gather.3.cloned.1.call-done), kind=kOutput, calls=%fused_computation.204 | convolution fusion | flops 1312604160 | bytes 14977024 | tf_op jit(solution)/shard_map/dot_general | solution.py:207
  216.0 54.7 %all-reduce.14.cloned.1.call-done = bf16[2352,512]{1,0:T(8,128)(2,1)} async-done(((bf16[2352,512]{1,0:T(8,128)(2,1)}), bf16[2352,512]{1,0:T(8,128)(2,1)}) %all-reduce.14.cloned.1.call-update) | async-done | bytes 2408464 | tf_op jit(solution)/shard_map/psum | solution.py:154
  278.6 9.8 copy.51
  333.1 16.8 %while.60 = (s32[]{:T(128)}, bf16[4,12,49,4,32]{2,4,3,1,0:T(8,128)(2,1)}, f32[4,12,4,49]{3,2,1,0:T(4,128)S(1)}, bf16[4,12,49,4,32]{2,4,3,1,0:T(8,128)(2,1)}, bf1...) while((s32[]{:T(128)}, ...), condition=%wide.region_13.14_spmd.clone, body=%wide.region_11.13_spmd.clone.sunk | while | flops 15420106 | bytes 3389057 | solution.py:195
  366.2 56.7 %all-reduce.16.cloned.1.call-done = bf16[2352,512]{1,0:T(8,128)(2,1)} async-done(((bf16[2352,512]{1,0:T(8,128)(2,1)}), bf16[2352,512]{1,0:T(8,128)(2,1)}) %all-reduce.16.cloned.1.call-update) | async-done | bytes 2408464 | tf_op jit(solution)/shard_map/psum | solution.py:154
  428.8 13.0 %multiply_convert_fusion = (bf16[2352,512]{1,0:T(8,128)(2,1)}, f32[2352,512]{1,0:T(8,128)S(1)}, f32[2352,512]{1,0:T(8,128)S(1)}) fusion(f32[512]{0:T(512)S(1)} %bitcast.502, bf16[2,512,512]{2,1,0:T(8,128)(2,1)S(1)} %copy-done.78, f32[2352,512]{1,0:T(8,128)S(1)} %get-tuple-element.468, f32[512]{0:T(512)S(1)} %bitcast.500, f32[512]{0:T(512)S(1)} %bitcast.472, ...), kind=kOutput, calls=%fused_computation.185 | convolution fusion | flops 1318625280 | bytes 17414144 | tf_op jit(solution)/shard_map/dot_general | solution.py:207
  460.8 45.7 %all-reduce.18.cloned.1.call-done = bf16[2352,512]{1,0:T(8,128)(2,1)} async-done(((bf16[2352,512]{1,0:T(8,128)(2,1)}), bf16[2352,512]{1,0:T(8,128)(2,1)}) %all-reduce.18.cloned.1.call-update) | async-done | bytes 2408464 | tf_op jit(solution)/shard_map/psum | solution.py:158
  538.8 43.6 %while.61 = (s32[]{:T(128)}, f32[4,12,49,4,32]{2,4,3,1,0:T(8,128)}, f32[4,12,49,4,32]{2,4,3,1,0:T(8,128)}, f32[4,12,49,4,32]{2,4,3,1,0:T(8,128)}, f32[4,4,49,49]...) while((s32[]{:T(128)}, f32[4,12,49,4,32]{2,4,3,1,0:T(8,128)}, ...), condition=%wide.region_24.25_spmd.clone, body=%wide.region_21.24_spmd.clone.sunk | while | flops 38184916 | bytes 9008673 | solution.py:303
  582.5 9.7 pad_maximum_fusion
  592.2 16.0 %copy.64 = f32[4,12,49,3,4,32]{5,4,3,1,0,2:T(4,128)} copy(f32[4,12,49,3,4,32]{2,5,4,1,0,3:T(8,128)} %pad_maximum_fusion) | data formatting | bytes 7225344 | tf_op jit(solution)/shard_map/stack | solution.py:308
  608.2 14.3 %reshape_reshape.36 = f32[12,2,2,7,7,384]{5,2,1,0,4,3:T(2,128)} reshape(f32[4,12,49,3,4,32]{5,4,3,1,0,2:T(4,128)} %copy.64) | data formatting | bytes 7225344 | tf_op jit(solution)/shard_map/reshape;reshape | solution.py:56
  665.8 41.7 %all-reduce.20.cloned.1.call-done = bf16[2352,512]{1,0:T(8,128)(2,1)} async-done(((bf16[2352,512]{1,0:T(8,128)(2,1)}), bf16[2352,512]{1,0:T(8,128)(2,1)}) %all-reduce.20.cloned.1.call-update) | async-done | bytes 2408464 | tf_op jit(solution)/shard_map/psum | solution.py:158
  734.4 49.7 %all-reduce.22.cloned.1.call-done = bf16[2352,512]{1,0:T(8,128)(2,1)} async-done(((bf16[2352,512]{1,0:T(8,128)(2,1)}), bf16[2352,512]{1,0:T(8,128)(2,1)}) %all-reduce.22.cloned.1.call-update) | async-done | bytes 2408464 | tf_op jit(solution)/shard_map/psum | solution.py:158
  819.0 50.4 %while.59 = (s32[]{:T(128)}, f32[4,12,49,4,32]{2,4,3,1,0:T(8,128)}, f32[4,12,49,4,32]{2,4,3,1,0:T(8,128)}, f32[4,12,49,4,32]{2,4,3,1,0:T(8,128)}, f32[4,4,49,49]...) while((s32[]{:T(128)}, f32[4,12,49,4,32]{2,4,3,1,0:T(8,128)}, ...), condition=%wide.region_34.35_spmd, body=%wide.region_31.34_spmd.sunk | while | flops 38050460 | bytes 7922665 | solution.py:303
  876.3 13.0 %copy.72 = bf16[4,12,49,3,4,32]{5,4,3,1,0,2:T(4,128)(2,1)} copy(bf16[4,12,49,3,4,32]{2,5,4,1,0,3:T(8,128)(2,1)} %fusion.101) | data formatting | bytes 3612672 | tf_op jit(solution)/shard_map/convert_element_type | solution.py:313
  889.4 11.8 %convert_element_type.276 = bf16[12,2,2,7,7,384]{5,2,1,0,4,3:T(2,128)(2,1)} reshape(bf16[4,12,49,3,4,32]{5,4,3,1,0,2:T(4,128)(2,1)} %copy.72) | data formatting | bytes 3612672 | tf_op jit(solution)/shard_map/convert_element_type | solution.py:313
  935.9 75.5 %all-reduce.26.cloned.1.call-done = (bf16[2352,512]{1,0:T(8,128)(2,1)}, bf16[2352,512]{1,0:T(8,128)(2,1)}) async-done(((bf16[2352,512]{1,0:T(8,128)(2,1)}, bf16[2352,512]{1,0:T(8,128)(2,1)}), (bf16[2352,512]{1,0:T(8,128)(2,1)}, bf16[2352,512]{1,0:T(8,128)(2,1)})) %all-reduce.26.cloned.1.call-update) | async-done | bytes 4816912 | tf_op jit(solution)/shard_map/psum | solution.py:158
  1015.9 39.2 %all-reduce = (bf16[2,3,128]{2,1,0:T(4,128)(2,1)S(1)}, bf16[2,512]{1,0:T(2,128)(2,1)S(1)}, bf16[2,512]{1,0:T(2,128)(2,1)S(1)}, bf16[2,169,4]{1,2,0:T(4,128)(2,1)...) all-reduce(bf16[2,3,128]{2,1,0:T(4,128)(2,1)S(1)} %fusion.198, ...), channel_id=1, replica_groups=mesh['dp'=4,'row'=2,'col'=4] {'dp','row'}, use_global_device_ids=true, to_apply=%region_48.49 | all-reduce | flops 9288 | bytes 37152 | tf_op jit(solution)/shard_map/psum | solution.py:345
  1073.2 72.3 %all-reduce.24.cloned.1.call-done = (bf16[2,512,3,128]{3,1,2,0:T(8,128)(2,1)}, bf16[2,512,128]{2,1,0:T(8,128)(2,1)}, bf16[2,512,512]{2,1,0:T(8,128)(2,1)}, bf16[2,512,512]{2,1,0:T(8,128)(2,1)}) async-done(((bf16[2,512,3,128]{3,1,2,0:T(8,128)(2,1)}, bf16[2,512,128]{2,1,0:T(8,128)(2,1)}, bf16[2,512,512]{2,1,0:T(8,128)(2,1)}, bf16[2,512,512]{2,1,0:T(8,128)(2,1)}), (bf16[2,512,3,128]{3,1,2,0:T(8,128)(2,1)}, ...) | async-done | bytes 3145744 | tf_op jit(solution)/shard_map/psum | solution.py:344
  (535 shorter events, 513.4 us)
Async XLA Ops:
  8.1 179.2 %all-reduce.12.cloned.1.call-start = ((), (), s32[]{:S(2)}) async-start(), calls=%async_computation | async-start | bytes 4816896 | tf_op jit(solution)/shard_map/psum | solution.py:154
  13.2 262.4 %copy-start.55 = (f32[1,512]{1,0:T(1,128)}, f32[1,512]{1,0:T(1,128)S(1)}, u32[]{:S(2)}) copy-start(f32[1,512]{1,0:T(1,128)S(1)} %get-tuple-element.496) | copy-start | bytes 6148
  26.0 249.5 %copy-start.75 = (f32[1,512]{1,0:T(1,128)}, f32[1,512]{1,0:T(1,128)S(1)}, u32[]{:S(2)}) copy-start(f32[1,512]{1,0:T(1,128)S(1)} %get-tuple-element.498) | copy-start | bytes 6148
  87.4 127.4 %copy-start.57 = (s32[2401]{0:T(1024)}, s32[2401]{0:T(1024)S(1)}, u32[]{:S(2)}) copy-start(s32[2401]{0:T(1024)S(1)} %eq.30) | copy-start | bytes 28816
  120.9 69.0 %copy-start.14 = (bf16[2352,128]{1,0:T(8,128)(2,1)}, bf16[2352,128]{1,0:T(8,128)(2,1)S(1)}, u32[]{:S(2)}) copy-start(bf16[2352,128]{1,0:T(8,128)(2,1)S(1)} %reshape.238) | copy-start | bytes 1806340
  129.0 65.4 %all-gather.3.cloned.1.call-start = ((), (), s32[]{:S(2)}) async-start(), calls=%async_computation.1 | async-start | bytes 1572864 | tf_op jit(solution)/shard_map/all_gather | solution.py:145
  129.6 79.5 %all-gather.5.cloned.1.call-start = ((), (), s32[]{:S(2)}) async-start(), calls=%async_computation.2 | async-start | bytes 1572864 | tf_op jit(solution)/shard_map/all_gather | solution.py:146
  130.2 140.5 %all-reduce.14.cloned.1.call-start = ((), (), s32[]{:S(2)}) async-start(), calls=%async_computation.3 | async-start | bytes 4816896 | tf_op jit(solution)/shard_map/psum | solution.py:154
  130.3 140.4 %copy-start.48 = (f32[1,512]{1,0:T(1,128)}, f32[1,512]{1,0:T(1,128)S(1)}, u32[]{:S(2)}) copy-start(f32[1,512]{1,0:T(1,128)S(1)} %get-tuple-element.500) | copy-start | bytes 6148
  130.3 61.0 %copy-start.50 = (f32[1,512]{1,0:T(1,128)}, f32[1,512]{1,0:T(1,128)S(1)}, u32[]{:S(2)}) copy-start(f32[1,512]{1,0:T(1,128)S(1)} %get-tuple-element.493) | copy-start | bytes 6148
  213.9 209.1 %all-reduce.16.cloned.1.call-start = ((), (), s32[]{:S(2)}) async-start(), calls=%async_computation.4 | async-start | bytes 4816896 | tf_op jit(solution)/shard_map/psum | solution.py:154
  363.9 62.9 %copy-start.16 = (bf16[2352,128]{1,0:T(8,128)(2,1)}, bf16[2352,128]{1,0:T(8,128)(2,1)S(1)}, u32[]{:S(2)}) copy-start(bf16[2352,128]{1,0:T(8,128)(2,1)S(1)} %reshape.243) | copy-start | bytes 1806340
  366.2 140.4 %all-reduce.18.cloned.1.call-start = ((), (), s32[]{:S(2)}) async-start(), calls=%async_computation.5 | async-start | bytes 4816896 | tf_op jit(solution)/shard_map/psum | solution.py:158
  449.7 257.7 %all-reduce.20.cloned.1.call-start = ((), (), s32[]{:S(2)}) async-start(), calls=%async_computation.6 | async-start | bytes 4816896 | tf_op jit(solution)/shard_map/psum | solution.py:158
  650.6 133.4 %all-reduce.22.cloned.1.call-start = ((), (), s32[]{:S(2)}) async-start(), calls=%async_computation.7 | async-start | bytes 4816896 | tf_op jit(solution)/shard_map/psum | solution.py:158
  727.2 284.2 %all-reduce.26.cloned.1.call-start = ((), (), s32[]{:S(2)}) async-start(), calls=%async_computation.9 | async-start | bytes 9633792 | tf_op jit(solution)/shard_map/psum | solution.py:158
  731.8 52.3 %copy-start.1 = (bf16[2352,512]{1,0:T(8,128)(2,1)S(1)}, bf16[2352,512]{1,0:T(8,128)(2,1)}, u32[]{:S(2)}) copy-start(bf16[2352,512]{1,0:T(8,128)(2,1)} %param.26) | copy-start | bytes 7225348
  731.8 52.3 %copy-start.37 = (f32[2352]{0:T(1024)S(1)}, f32[2352]{0:T(1024)}, u32[]{:S(2)}) copy-start(f32[2352]{0:T(1024)} %copy-done.36) | copy-start | bytes 28228
  731.8 52.3 %copy-start.41 = (f32[2352]{0:T(1024)S(1)}, f32[2352]{0:T(1024)}, u32[]{:S(2)}) copy-start(f32[2352]{0:T(1024)} %copy-done.40) | copy-start | bytes 28228
  731.8 52.3 %copy-start.49 = (f32[1,512]{1,0:T(1,128)S(1)}, f32[1,512]{1,0:T(1,128)}, u32[]{:S(2)}) copy-start(f32[1,512]{1,0:T(1,128)} %copy-done.48) | copy-start | bytes 6148
  731.8 52.3 %copy-start.51 = (f32[1,512]{1,0:T(1,128)S(1)}, f32[1,512]{1,0:T(1,128)}, u32[]{:S(2)}) copy-start(f32[1,512]{1,0:T(1,128)} %copy-done.50) | copy-start | bytes 6148
  915.6 229.9 %all-reduce.24.cloned.1.call-start = ((), (), s32[]{:S(2)}) async-start(), calls=%async_computation.8 | async-start | bytes 6291456 | tf_op jit(solution)/shard_map/psum | solution.py:344
  934.8 81.0 %copy-start.62 = (f32[512]{0:T(512)S(1)}, f32[512]{0:T(512)}, u32[]{:S(2)}) copy-start(f32[512]{0:T(512)} %get-tuple-element.361) | copy-start | bytes 6148
  934.8 125.6 %copy-start.59 = (f32[1,512]{1,0:T(1,128)S(1)}, f32[1,512]{1,0:T(1,128)}, u32[]{:S(2)}) copy-start(f32[1,512]{1,0:T(1,128)} %get-tuple-element.488) | copy-start | bytes 6148
  (85 other events, 585.3 us)
Sparse Core Ops, SparseCore 0:
  129.2 58.0 all-reduce.11
  214.0 56.6 all-reduce.13
  366.3 56.6 all-reduce.15
  449.9 56.6 all-reduce.17
  650.8 56.6 all-reduce.19
  727.4 56.6 all-reduce.21
  915.8 95.6 all-reduce.25
  1015.9 129.5 all-reduce.23
Sparse Core Ops, SparseCore 1:
  131.1 22.6 all-gather.2
  155.1 21.1 all-gather.4
where the time goes:
time: 1180 us; the launch traced here: 1160 us
  waiting for transfers between devices  454 us (38%)
  local copies, waits for them, and re-layouts  281 us (24%)
  matrix products  211 us (18%)
  other arithmetic  138 us (12%)
  blocking collectives  57.8 us (5%)
  between operations  17.6 us (1%)
    psum x4, waiting for transfers between devices, back_sum(): lax.psum(partial_value.astype(jnp.bfloat16), 'col').astype(jnp.float32)  213 us
    psum x3, waiting for transfers between devices, out_sum(): lax.psum(partial_value.astype(jnp.bfloat16), 'col').astype(jnp.float32)  168 us
    psum x1, waiting for transfers between devices, shards(): lax.psum(stacked_grads[2].astype(jnp.bfloat16), ('dp', 'row'))  72.3 us
    convert_element_type x5, local copies, waits for them, and re-layouts, shards(): triple_low_grad = triple_grad.astype(jnp.bfloat16)  40.5 us
    psum x1, blocking collectives, shards(): lax.psum(stacked_grads[3].astype(jnp.bfloat16), ('dp', 'row'))  39.2 us
    unnamed x205, local copies, waits for them, and re-layouts  31.8 us
    while x5, local copies, waits for them, and re-layouts, shards(): lax.map(forward_block, (query_blk, key_blk, value_blk))  31.5 us
    dot_general x2, matrix products, shards(): jnp.dot(second_low, expand_full[layer_index], preferred_element_type=jnp....  27.7 us
  transfers between devices with their start and end apart: 10, of which 8 were waited for; matrix products, arithmetic and copies ran while one was open for 9% of the time, Pallas kernels for 0%

commit v1 on v0

v1 whole, which is shorter than its diff:
```python
import functools
import math

import jax
import jax.numpy as jnp
from jax import lax
from jax.experimental import pallas as pl
from jax.experimental.pallas import tpu as pltpu
from jax.sharding import PartitionSpec as P

LAYERS = 2
SIDE = 14
WIN = 7
SHIFT = 3
HEAD = 32
RELS = 169
EPSILON = 1e-05
MASKED = -100.0
GONE = -1e30
CELLS = WIN * WIN
ROWS = 56
SLOT = 64
GROUP = 4
LANES = 128
WIDE = GROUP * SLOT
F32 = jnp.float32
BF16 = jnp.bfloat16
ROOT_HALF = 1.0 / math.sqrt(2.0)
GAUSS = 1.0 / math.sqrt(2.0 * math.pi)


def mm(a, b):
    return lax.dot_general(a, b, (((1,), (0,)), ((), ())), preferred_element_type=F32)


def mm_nt(a, b):
    return lax.dot_general(a, b, (((1,), (1,)), ((), ())), preferred_element_type=F32)


def mm_tn(a, b):
    return lax.dot_general(a, b, (((0,), (0,)), ((), ())), preferred_element_type=F32)


def loop(count, body):
    def step(index, carry):
        body(index)
        return carry

    lax.fori_loop(0, count, step, 0)


def span(index, size):
    return pl.ds(pl.multiple_of(index * size, size), size)


def fold(values):
    rows, columns = values.shape
    return jnp.sum(values.reshape(rows // 8, 8, columns), axis=0)


def order(images, shift):
    found = {}
    for image in range(images):
        for wi in range(2):
            for wj in range(2):
                window = image * 4 + wi * 2 + wj
                for a in range(WIN):
                    for b in range(WIN):
                        i = (wi * WIN + a + shift) % SIDE
                        j = (wj * WIN + b + shift) % SIDE
                        found[window * ROWS + a * WIN + b] = image * SIDE * SIDE + i * SIDE + j
    return found


def runs(pairs):
    joined = []
    for to, source in sorted(pairs):
        if joined and joined[-1][0] + joined[-1][2] == to and joined[-1][1] + joined[-1][2] == source:
            joined[-1][2] += 1
        else:
            joined.append([to, source, 1])
    return joined


def image_to_window(images, shift):
    return runs(order(images, shift).items())


def window_to_image(images, shift):
    return runs((source, to) for to, source in order(images, shift).items())


def window_to_window(images, before, after):
    at = {token: row for row, token in order(images, before).items()}
    return runs((row, at[token]) for row, token in order(images, after).items())


def move_rows(target, source, moves):
    for to, start, length in moves:
        target[pl.ds(to, length), :] = source[pl.ds(start, length), :]


def norm_rows(hidden, gain, offset):
    average = jnp.mean(hidden, axis=-1, keepdims=True)
    centered = hidden - average
    variance = jnp.mean(centered * centered, axis=-1, keepdims=True)
    inverse = lax.rsqrt(variance + EPSILON)
    normed = centered * inverse
    return normed * gain + offset, normed, inverse


def spread(block, mask):
    return jnp.concatenate([block] * GROUP, axis=0) * mask


def gather_heads(stacked, lane):
    out = stacked[(GROUP - 1) * SLOT :]
    for head in reversed(range(GROUP - 1)):
        out = jnp.where(lane < (head + 1) * HEAD, stacked[head * SLOT : (head + 1) * SLOT], out)
    return out


def padded(rows):
    return jnp.concatenate([rows, jnp.zeros((SLOT - ROWS, rows.shape[1]), rows.dtype)], axis=0).astype(BF16)


class Sizes:
    def __init__(self, images, width, hidden):
        self.images = images
        self.windows = images * 4
        self.tokens = self.windows * ROWS
        self.width = width
        self.hidden = hidden
        self.groups = width // LANES
        self.pairs = self.windows // 2
        self.chunk = self.tokens // 2
        self.third = self.tokens // 3


def forward_norm(sz, hidden, gain, offset, low, hat, inv):
    def body(i):
        at = span(i, 2 * ROWS)
        normed, centered, inverse = norm_rows(hidden[at, :], gain, offset)
        low[at, :] = normed.astype(BF16)
        hat[at, :] = centered.astype(BF16)
        inv[at, :] = inverse

    loop(sz.pairs, body)


def forward_triple(sz, low, weight, bias, outs):
    per = sz.chunk // ROWS
    for part in range(3):

        def body(i, part=part):
            acc = mm(low[span(i, sz.chunk), :], weight[part]) + bias[part : part + 1, :]
            if part == 0:
                acc = acc * HEAD ** (-0.5)
            for j in range(per):
                outs[part][i * per + j] = padded(acc[j * ROWS : (j + 1) * ROWS])

        loop(2, body)


def forward_attend(sz, parts, bias, mask, heads, ones, probs, out_slots, out_rows):
    query, key, value = parts

    def body(pair):
        for group in range(sz.groups):
            cols = slice(group * LANES, (group + 1) * LANES)
            halves = []
            for half in range(2):
                window = pair * 2 + half
                scores = mm_nt(query[window, :, cols], spread(key[window, :, cols], heads[...])) + bias[group]
                if mask is not None:
                    scores = scores + mask[lax.rem(window, 4)]
                grown = jnp.exp(scores)
                high = grown.astype(BF16)
                low = (grown - high.astype(F32)).astype(BF16)
                total = mm(high, ones[...]) + mm(low, ones[...])
                prob = jnp.exp(scores - jnp.log(total)).astype(BF16)
                probs[window, group] = prob
                out = mm(prob, spread(value[window, :, cols], heads[...]))
                out_slots[window, :, cols] = out.astype(BF16)
                halves.append(out[:ROWS])
            out_rows[span(pair, 2 * ROWS), cols] = jnp.concatenate(halves, axis=0).astype(BF16)

    loop(sz.pairs, body)


def add_product(sz, hidden, left, weight, bias):
    def body(i):
        at = span(i, sz.chunk)
        hidden[at, :] = hidden[at, :] + mm_nt(left[at, :], weight[...]) + bias

    loop(2, body)


def forward_expand(sz, low, weight, bias, act, slope):
    parts = sz.hidden // sz.width

    def body(i):
        rows = span(i // parts, sz.third)
        cols = span(lax.rem(i, parts), sz.width)
        u = mm(low[rows, :], weight[:, cols]) + bias[:, cols]
        phi = 0.5 + 0.5 * lax.erf(u * ROOT_HALF)
        act[rows, cols] = (u * phi).astype(BF16)
        slope[rows, cols] = (phi + u * (GAUSS * jnp.exp(-0.5 * u * u))).astype(BF16)

    loop(3 * parts, body)


def backward_norm(sz, upstream, grad, hat, inv, gain, sums):
    def body(i):
        at = span(i, 2 * ROWS)
        up = upstream[at, :]
        normed = hat[at, :].astype(F32)
        weighted = up * gain
        first = jnp.mean(weighted, axis=-1, keepdims=True)
        second = jnp.mean(weighted * normed, axis=-1, keepdims=True)
        grad[at, :] = grad[at, :] + inv[at, :] * (weighted - first - normed * second)
        sums[0] += fold(up * normed)
        sums[1] += fold(up)

    sums[0] = jnp.zeros_like(sums[0])
    sums[1] = jnp.zeros_like(sums[1])
    loop(sz.pairs, body)


def round_grad(sz, grad, low, low_t, total):
    total[...] = jnp.zeros_like(total)

    def body(i):
        at = span(i, 2 * ROWS)
        values = grad[at, :]
        low[at, :] = values.astype(BF16)
        total[...] += fold(values)

    loop(sz.pairs, body)


def backward_hidden(sz, grad_low, weight, slope, pre_low, total):
    parts = sz.hidden // sz.width
    total[...] = jnp.zeros_like(total)

    def body(i):
        rows = span(i // parts, sz.third)
        cols = span(lax.rem(i, parts), sz.width)
        pre = mm(grad_low[rows, :], weight[:, cols]) * slope[rows, cols].astype(F32)
        pre_low[rows, cols] = pre.astype(BF16)
        total[:, cols] += fold(pre)

    loop(3 * parts, body)


def weight_grad(parts, left, right, width, out, scale):
    def body(i):
        cols = span(i, width)
        out[:, cols] = (mm_tn(left[...], right[:, cols]) * scale).astype(out.dtype)

    loop(parts, body)


def backward_out(sz, grad_low, weight, out_slots):
    per = sz.chunk // ROWS

    def body(i):
        acc = mm(grad_low[span(i, sz.chunk), :], weight[...])
        for j in range(per):
            out_slots[i * per + j] = padded(acc[j * ROWS : (j + 1) * ROWS])

    loop(2, body)


def backward_attend(sz, parts, probs, out_slots, grad_slots, heads, lane, outs, totals, score_sum):
    query, key, value = parts
    for group in range(sz.groups):
        score_sum[group] = jnp.zeros_like(score_sum[group])
    totals[...] = jnp.zeros_like(totals)

    def body(pair):
        for group in range(sz.groups):
            cols = slice(group * LANES, (group + 1) * LANES)
            halves = [[], [], []]
            for half in range(2):
                window = pair * 2 + half
                q, k, v = query[window, :, cols], key[window, :, cols], value[window, :, cols]
                prob = probs[window, group]
                grad = grad_slots[window, :, cols]
                inner = -(grad.astype(F32) * out_slots[window, :, cols].astype(F32))
                left = jnp.concatenate([grad, inner.astype(BF16)], axis=1)
                right = jnp.concatenate([spread(v, heads[...]), heads[...]], axis=1)
                score = prob.astype(F32) * mm_nt(left, right)
                score_sum[group] += score
                score_low = score.astype(BF16)
                halves[0].append((mm(score_low, spread(k, heads[...])) * HEAD ** (-0.5))[:ROWS])
                halves[1].append(gather_heads(mm_tn(score_low, q), lane)[:ROWS])
                halves[2].append(gather_heads(mm_tn(prob, grad), lane)[:ROWS])
            for part in range(3):
                joined = jnp.concatenate(halves[part], axis=0)
                outs[part, span(pair, 2 * ROWS), cols] = joined.astype(BF16)
                totals[part, :, cols] += fold(joined)

    loop(sz.pairs, body)


def back_product(sz, lefts, weights, out):
    def body(i):
        at = span(i, sz.chunk)
        total = mm_nt(lefts[0][at, :], weights[0][...])
        for left, weight in zip(lefts[1:], weights[1:]):
            total = total + mm_nt(left[at, :], weight[...])
        out[at, :] = total

    loop(2, body)


def to_windows(tokens, images, offset):
    blocks = SIDE // WIN
    columns = tokens.shape[-1]
    spatial = tokens.reshape(images, SIDE, SIDE, columns)
    if offset:
        spatial = jnp.roll(spatial, (-offset, -offset), axis=(1, 2))
    spatial = spatial.reshape(images, blocks, WIN, blocks, WIN, columns).transpose(0, 1, 3, 2, 4, 5)
    return spatial.reshape(images * blocks * blocks, WIN * WIN, columns)


def region_mask(region_ids):
    cells = to_windows(region_ids.reshape(SIDE * SIDE, 1), 1, 0)[:, :, 0]
    return jnp.where(cells[:, :, None] == cells[:, None, :], 0.0, MASKED).astype(jnp.float32)


def rel_onehot(rel_index):
    return (rel_index.reshape(-1)[:, None] == jnp.arange(RELS, dtype=jnp.int32)[None, :]).astype(jnp.float32)


def rel_bias(onehot, table):
    count = table.shape[1]
    return jnp.dot(onehot, table, precision=lax.Precision.HIGHEST).T.reshape(count, WIN * WIN, WIN * WIN)


def head_mask():
    row = lax.broadcasted_iota(jnp.int32, (WIDE, LANES), 0) // SLOT
    col = lax.broadcasted_iota(jnp.int32, (WIDE, LANES), 1) // HEAD
    return jnp.where(row == col, 1.0, 0.0).astype(BF16)

def ones_mask():
    row = lax.broadcasted_iota(jnp.int32, (WIDE, WIDE), 0) // SLOT
    col = lax.broadcasted_iota(jnp.int32, (WIDE, WIDE), 1) // SLOT
    return jnp.where(row == col, 1.0, 0.0).astype(BF16)

def forward_kernel(sz, x, wt, wp, we, wr, fg, fo, tb, pb, sg, so, eb, rb, bias, mask, heads, ones,
                   out, n1, xh1, r1, q, k, v, probs, o64, oc, n2, xh2, r2, gp, act, ha, hb):
    move = [image_to_window(sz.images, 0), window_to_window(sz.images, 0, SHIFT), window_to_image(sz.images, SHIFT)]
    hb[...] = jnp.zeros_like(hb)
    ha[...] = jnp.zeros_like(ha)
    hb[0:592, :] = x[...].astype(F32)
    move_rows(ha, hb, move[0])
    bufs = [ha, hb]
    for l in range(2):
        h = bufs[l]
        forward_norm(sz, h, fg[l:l+1, :], fo[l:l+1, :], n1.at[l], xh1.at[l], r1.at[l])
        forward_triple(sz, n1.at[l], wt.at[l], tb.at[l], (q.at[l], k.at[l], v.at[l]))
        forward_attend(sz, (q.at[l], k.at[l], v.at[l]), bias.at[l], mask if l else None, heads, ones, probs.at[l], o64.at[l], oc.at[l])
        add_product(sz, h, oc.at[l], wp.at[l], pb[l:l+1, :])
        forward_norm(sz, h, sg[l:l+1, :], so[l:l+1, :], n2.at[l], xh2.at[l], r2.at[l])
        forward_expand(sz, n2.at[l], we.at[l], eb.at[l:l+1], act.at[l], gp.at[l])
        add_product(sz, h, act.at[l], wr.at[l], rb[l:l+1, :])
        if l == 0:
            hb[...] = jnp.zeros_like(hb)
            move_rows(hb, ha, move[1])
        else:
            move_rows(ha, hb, move[2])
            out[...] = ha[0:592, :]

def backward_kernel(sz, scale, which, cot, wt, wp, we, wr, fg, sg, heads, n1, xh1, r1, q, k, v, probs, o64, oc, n2, xh2, r2, gp, act,
                    out, gt, gp_, ge, gr, small, big, tsum, ssum, ga, gb, low, pre, dn, do64, dc, sums):
    move = [image_to_window(sz.images, SHIFT), window_to_window(sz.images, SHIFT, 0), window_to_image(sz.images, 0)]
    ga[...] = jnp.zeros_like(ga); gb[...] = jnp.zeros_like(gb)
    if which:
        ga[0:592, :] = cot[...].astype(F32)
        move_rows(gb, ga, move[0])
    else:
        gb[...] = cot[...]
    lane = lax.broadcasted_iota(jnp.int32, (SLOT, LANES), 1)
    l = 0
    e = gb
    round_grad(sz, e, low, None, small.at[l, 0])
    weight_grad(4, low, act.at[l], sz.width, gr.at[l], scale)
    backward_hidden(sz, low, wr.at[l], gp.at[l], pre, big.at[l])
    weight_grad(4, n2.at[l], pre, sz.width, ge.at[l], scale)
    back_product(sz, [pre], [we.at[l]], dn)
    backward_norm(sz, dn, e, xh2.at[l], r2.at[l], sg[l:l+1, :], small.at[l, 1:3])
    round_grad(sz, e, low, None, small.at[l, 3])
    weight_grad(1, low, oc.at[l], sz.width, gp_.at[l], scale)
    backward_out(sz, low, wp.at[l], do64)
    backward_attend(sz, (q.at[l], k.at[l], v.at[l]), probs.at[l], o64.at[l], do64, heads, lane, dc, tsum.at[l], ssum.at[l])
    for part in range(3):
        weight_grad(1, n1.at[l], dc.at[part], sz.width, gt.at[l, part], scale)
    back_product(sz, [dc.at[p] for p in range(3)], [wt.at[l, p] for p in range(3)], dn)
    backward_norm(sz, dn, e, xh1.at[l], r1.at[l], fg[l:l+1, :], small.at[l, 4:6])
    ga[...] = jnp.zeros_like(ga)
    if which:
        move_rows(ga, gb, move[1])
        out[...] = ga[...]
    else:
        move_rows(ga, gb, move[2])
        out[...] = ga[...]

LIMIT = 66_900_000
def saved_shapes(sz):
    L, T, D, W = 2, sz.tokens, sz.width, sz.windows
    return [((L,T,D),BF16),((L,T,D),BF16),((L,T,1),F32),((L,W,SLOT,D),BF16),((L,W,SLOT,D),BF16),((L,W,SLOT,D),BF16),
            ((L,W,sz.groups,SLOT,WIDE),BF16),((L,W,SLOT,D),BF16),((L,T,D),BF16),((L,T,D),BF16),((L,T,D),BF16),((L,T,1),F32),
            ((L,T,sz.hidden),BF16),((L,T,sz.hidden),BF16)]
VM = pl.BlockSpec(memory_space=pltpu.VMEM)

def fwd_call(sz, *args):
    shapes = [((592, sz.width), F32)] + saved_shapes(sz)
    return pl.pallas_call(functools.partial(forward_kernel, sz),
        out_shape=[jax.ShapeDtypeStruct(s, d) for s, d in shapes],
        in_specs=[VM]*len(args), out_specs=[VM]*len(shapes),
        scratch_shapes=[pltpu.VMEM((sz.tokens, sz.width), F32)]*2,
        compiler_params=pltpu.CompilerParams(vmem_limit_bytes=LIMIT), name="fwd")(*args)

def bwd_one(sz, scale, which, *args):
    L,D,T,F = 1, sz.width, sz.tokens, sz.hidden
    shapes = [((T,D),F32), ((L,3,D,D),BF16), ((L,D,D),BF16), ((L,D,F),BF16), ((L,D,F),BF16), ((L,6,8,D),F32), ((L,8,F),F32), ((L,3,8,D),F32), ((L,sz.groups,SLOT,WIDE),F32)]
    return pl.pallas_call(functools.partial(backward_kernel, sz, scale, which),
        out_shape=[jax.ShapeDtypeStruct(s, d) for s, d in shapes],
        in_specs=[VM]*len(args), out_specs=[VM]*len(shapes),
        scratch_shapes=[pltpu.VMEM((T,D),F32)]*2+[pltpu.VMEM((T,D),BF16), pltpu.VMEM((T,F),BF16), pltpu.VMEM((T,D),F32), pltpu.VMEM((sz.windows,SLOT,D),BF16), pltpu.VMEM((3,T,D),BF16), pltpu.VMEM((8,128),F32)],
        compiler_params=pltpu.CompilerParams(vmem_limit_bytes=LIMIT), name="bwd%d"%which)(*args)

def bwd_call(sz, scale, cot, *args):
    one = lambda which, c: bwd_one(sz, scale, which, c, *[a if a.shape[0] != 2 else a[which:which+1] for a in args])
    b = one(1, cot)
    c = one(0, b[0])
    return [c[0][:592]] + [jnp.concatenate([x, y], 0) for x, y in zip(c[1:], b[1:])]


def shards(
    block_input, cotangent, region_ids, rel_index, first_gain, first_offset, triple_weight, triple_bias, rel_table,
    project_weight, project_bias, second_gain, second_offset, expand_weight, expand_bias, reduce_weight, reduce_bias,
):
    cols = lax.axis_size("col")
    tokens = block_input.shape[0]
    mine = tokens // cols
    scale = 1.0 / math.sqrt(tokens * lax.axis_size("dp") * lax.axis_size("row"))
    sz = Sizes(mine // (SIDE * SIDE), block_input.shape[1], expand_weight.shape[2] * cols)
    held = -(-mine // 16) * 16
    start = lax.axis_index("col") * mine

    def whole(weight, last):
        return lax.all_gather(lax.all_gather(weight, "row", axis=1, tiled=True), "col", axis=last, tiled=True)

    wt = jnp.transpose(whole(triple_weight, 3), (0, 2, 1, 3))
    wp, we, wr = whole(project_weight, 2), whole(expand_weight, 2), whole(reduce_weight, 2)
    tb = lax.all_gather(triple_bias, "col", axis=2, tiled=True)
    eb = lax.all_gather(expand_bias, "col", axis=1, tiled=True)
    table = lax.all_gather(rel_table, "col", axis=2, tiled=True)
    cut = lambda rows: jnp.pad(lax.dynamic_slice_in_dim(rows, start, mine, 0), ((0, held - mine), (0, 0)))
    onehot = rel_onehot(rel_index)
    bias = jnp.stack([rel_bias(onehot, table[layer]) for layer in range(LAYERS)])
    bias = jnp.pad(bias, ((0, 0), (0, 0), (0, SLOT - CELLS), (0, 0)))
    bias = jnp.pad(bias, ((0, 0), (0, 0), (0, 0), (0, SLOT - CELLS)), constant_values=GONE)
    bias = bias.reshape(LAYERS, sz.groups, GROUP, SLOT, SLOT).transpose(0, 1, 3, 2, 4)
    bias = bias.reshape(LAYERS, sz.groups, SLOT, WIDE)
    mask = jnp.pad(region_mask(region_ids), ((0, 0), (0, SLOT - CELLS), (0, SLOT - CELLS)))
    mask = jnp.tile(mask, (1, 1, GROUP))
    heads = head_mask()
    saved = fwd_call(
        sz, cut(block_input), wt, wp, we, wr, first_gain, first_offset, tb, project_bias, second_gain, second_offset, eb,
        reduce_bias, bias, mask, heads, ones_mask(),
    )
    back = bwd_call(
        sz, scale, cut(cotangent), wt, wp, we, wr, first_gain, second_gain, heads, *saved[1:]
    )

    def rows_out(rows):
        return lax.all_gather(rows[:mine].astype(BF16), "col", axis=0, tiled=True).astype(F32)

    def scatter(grad, last):
        grad = lax.psum_scatter(grad, "row", scatter_dimension=1, tiled=True)
        grad = lax.psum_scatter(grad, "col", scatter_dimension=last, tiled=True)
        return lax.psum(grad, "dp").astype(F32)

    gt = scatter(jnp.transpose(back[1], (0, 2, 1, 3)), 3)
    gp, ge, gr = scatter(back[2], 2), scatter(back[3], 2), scatter(back[4], 2)
    small = jnp.sum(back[5], axis=2) * scale
    big = jnp.sum(back[6], axis=1) * scale
    tsum = jnp.sum(back[7], axis=2) * scale
    ssum = back[8].reshape(LAYERS, sz.groups, SLOT, GROUP, SLOT)[:, :, :CELLS, :, :CELLS]
    ssum = ssum.transpose(0, 1, 3, 2, 4).reshape(LAYERS, sz.groups * GROUP, CELLS * CELLS)
    gtab = jnp.einsum("lhp,pm->lmh", ssum, onehot, precision=lax.Precision.HIGHEST) * scale
    small, big, tsum, gtab = lax.psum((small, big, tsum, gtab), ("dp", "row", "col"))
    own = lambda value, axis: lax.dynamic_slice_in_dim(
        value, lax.axis_index("col") * (value.shape[axis] // cols), value.shape[axis] // cols, axis
    )
    return (
        rows_out(saved[0]), rows_out(back[0]), small[:, 4], small[:, 5], gt, own(tsum, 2), own(gtab, 2), gp, small[:, 3],
        small[:, 1], small[:, 2], ge, own(big, 1), gr, small[:, 0],
    )


def solution(mesh):
    specs = (
        P(("dp", "row"), None), P(("dp", "row"), None), P(), P(), P(), P(), P(None, "row", None, "col"), P(None, None, "col"),
        P(None, None, "col"), P(None, "row", "col"), P(), P(), P(), P(None, "row", "col"), P(None, "col"),
        P(None, "row", "col"), P(),
    )
    outs = specs[:2] + (
        P(), P(), P(None, "row", None, "col"), P(None, None, "col"), P(None, None, "col"), P(None, "row", "col"), P(), P(), P(),
        P(None, "row", "col"), P(None, "col"), P(None, "row", "col"), P(),
    )
    return jax.shard_map(shards, mesh=mesh, in_specs=specs, out_specs=outs, check_vma=False)
```

time: 1180 us -> 950 us (0.81); the launches traced: 1160 us -> 944 us
  matrix products: 211 us -> 2.94 us
  local copies, waits for them, and re-layouts: 281 us -> 84 us
  waiting for transfers between devices: 454 us -> 623 us
  Pallas kernels: 0 us -> 150 us
  other arithmetic: 138 us -> 22.2 us
  blocking collectives: 57.8 us -> 45.6 us
    psum x8 -> x2, waiting for transfers between devices: 453 us -> 200 us  [the longest x1 131 us: shards(): lax.psum((small, big, tsum, gtab), ('dp', 'row', 'col'))]
    reduce_scatter x0 -> x6, waiting for transfers between devices: none -> 223 us  [the longest x4 159 us: scatter(): grad = lax.psum_scatter(grad, 'row', scatter_dimension=1, tiled=True)]
    dot_general x84 -> x3, matrix products: 211 us -> 2.94 us  [the longest x1 1.61 us: shards(): jnp.einsum('lhp,pm->lmh', ssum, onehot, precision=lax.Precision.HIGHEST)]
    all_gather x2 -> x8, waiting for transfers between devices: 0.01 us -> 154 us  [the longest x4 85.6 us: whole(): lax.all_gather(lax.all_gather(weight, 'row', axis=1, tiled=True), 'col',...]
    pallas_call x0 -> x3, Pallas kernels: none -> 150 us  [the longest x2 79.8 us: bwd_one(): pl.pallas_call(functools.partial(backward_kernel, sz, scale, which), out_...]
    another operation x24 -> x4, local copies, waits for them, and re-layouts: 85.3 us -> 1.54 us  [the longest x2 1.14 us: shards(): mask = jnp.tile(mask, (1, 1, GROUP))]
    reduce_sum x29 -> x3, other arithmetic: 79.8 us -> 0.14 us  [the longest x1 0.05 us: shards(): small = jnp.sum(back[5], axis=2) * scale]
    convert_element_type x7 -> x2, local copies, waits for them, and re-layouts: 60.6 us -> 7.45 us  [rows_out(): lax.all_gather(rows[:mine].astype(BF16), 'col', axis=0, tiled=True)]
  transfers between devices with their start and end apart: 10 -> 18, of which waited for: 8 -> 17; matrix products, arithmetic and copies ran while one was open for 9% -> 7% of each run, Pallas kernels for 0% -> 0%
where the time goes in v1:
time: 950 us; the launch traced here: 944 us
  waiting for transfers between devices  623 us (66%)
  Pallas kernels  150 us (16%)
  local copies, waits for them, and re-layouts  84 us (9%)
  blocking collectives  45.6 us (5%)
  other arithmetic  22.2 us (2%)
  between operations  15 us (2%)
    reduce_scatter x4, waiting for transfers between devices, scatter(): grad = lax.psum_scatter(grad, 'row', scatter_dimension=1, tiled=True)  159 us
    psum x1, waiting for transfers between devices, shards(): lax.psum((small, big, tsum, gtab), ('dp', 'row', 'col'))  131 us
    all_gather x4, waiting for transfers between devices, whole(): lax.all_gather(lax.all_gather(weight, 'row', axis=1, tiled=True), 'col',...  85.6 us
    pallas_call x2, Pallas kernels, bwd_one(): pl.pallas_call(functools.partial(backward_kernel, sz, scale, which), out_...  79.8 us
    pallas_call x1, Pallas kernels, fwd_call(): pl.pallas_call(functools.partial(forward_kernel, sz), out_shape=[jax.Shap...  70.1 us
    psum x1, waiting for transfers between devices, scatter(): return lax.psum(grad, 'dp').astype(F32)  69 us
    reduce_scatter x2, waiting for transfers between devices, scatter(): grad = lax.psum_scatter(grad, 'col', scatter_dimension=last, tiled=True)  64.5 us
    unnamed x20, waiting for transfers between devices  46.6 us
  transfers between devices with their start and end apart: 18, of which 17 were waited for; matrix products, arithmetic and copies ran while one was open for 7% of the time, Pallas kernels for 0%

profile of v1, /device:TPU:0, one launch (start us, length us, event | category | flops | bytes accessed | tf_op | source)
XLA Modules:
  0.0 943.8 jit_solution(8436377022915178304)
XLA Ops:
  8.7 9.0 all_gather.41
  17.8 20.2 %all_gather.39 = bf16[2,512,3,128]{3,1,2,0:T(8,128)(2,1)} all-gather(bf16[2,256,3,128]{3,1,2,0:T(8,128)(2,1)} %param.23), channel_id=1, replica_groups=mesh['dp'=4,'row'=2,'col'=4] {'row'}, dimensions={1}, use_global_device_ids=true | all-gather | bytes 1179648 | tf_op jit(solution)/shard_map/all_gather | solution.py:455
  40.5 24.3 %all-gather.19.cloned.1.call-done = bf16[2,512,512]{2,1,0:T(8,128)(2,1)} async-done(((bf16[2,256,512]{2,1,0:T(8,128)(2,1)}), bf16[2,512,512]{2,1,0:T(8,128)(2,1)}) %all-gather.19.cloned.1.call-update) | async-done | bytes 1048592 | tf_op jit(solution)/shard_map/all_gather | solution.py:455
  80.1 5.6 all_gather.47.tb
  85.7 5.6 all_gather.48.eb
  95.8 17.8 %all-gather.11.cloned.1.call-done = bf16[2,512,3,512]{3,1,2,0:T(8,128)(2,1)} async-done(((bf16[2,512,3,128]{3,1,2,0:T(8,128)(2,1)}), bf16[2,512,3,512]{3,1,2,0:T(8,128)(2,1)}) %all-gather.11.cloned.1.call-update) | async-done | bytes 3145744 | tf_op jit(solution)/shard_map/all_gather | solution.py:455
  117.6 31.9 %all-gather.17.cloned.1.call-done.we = bf16[2,512,2048]{2,1,0:T(8,128)(2,1)} async-done(((bf16[2,512,512]{2,1,0:T(8,128)(2,1)}), bf16[2,512,2048]{2,1,0:T(8,128)(2,1)}) %all-gather.17.cloned.1.call-update) | async-done | bytes 4194320 | tf_op jit(solution)/shard_map/all_gather | solution.py:455
  149.5 35.9 %all-gather.21.cloned.1.call-done.wr = bf16[2,512,2048]{2,1,0:T(8,128)(2,1)} async-done(((bf16[2,512,512]{2,1,0:T(8,128)(2,1)}), bf16[2,512,2048]{2,1,0:T(8,128)(2,1)}) %all-gather.21.cloned.1.call-update) | async-done | bytes 4194320 | tf_op jit(solution)/shard_map/all_gather | solution.py:455
  185.4 70.1 %fwd.1 = (f32[592,512]{1,0:T(8,128)}, bf16[2,672,512]{2,1,0:T(8,128)(2,1)}, bf16[2,672,512]{2,1,0:T(8,128)(2,1)}, f32[2,672,1]{2,1,0:T(8,128)}, bf16[2,12,64,512...) custom-call(bf16[592,512]{1,0:T(8,128)(2,1)} %pad.19.x, ...), custom_call_target="tpu_custom_call" | custom-call | tf_op jit(solution)/shard_map/fwd/pallas_call | solution.py:420
  255.5 6.1 fusion.18
  287.9 40.0 %bwd1.1 = (f32[672,512]{1,0:T(8,128)}, bf16[1,3,512,512]{3,2,1,0:T(8,128)(2,1)}, bf16[1,512,512]{2,1,0:T(8,128)(2,1)}, bf16[1,512,2048]{2,1,0:T(8,128)(2,1)}, bf...) custom-call(bf16[592,512]{1,0:T(8,128)(2,1)} %pad.23.cot, ...), custom_call_target="tpu_custom_call" | custom-call | tf_op jit(solution)/shard_map/bwd1/pallas_call | solution.py:429
  327.9 39.8 %bwd0.1 = (f32[672,512]{1,0:T(8,128)}, bf16[1,3,512,512]{3,2,1,0:T(8,128)(2,1)}, bf16[1,512,512]{2,1,0:T(8,128)(2,1)}, bf16[1,512,2048]{2,1,0:T(8,128)(2,1)}, bf...) custom-call(f32[672,512]{1,0:T(8,128)} %get-tuple-element.63.cot, ...), custom_call_target="tpu_custom_call" | custom-call | tf_op jit(solution)/shard_map/bwd0/pallas_call | solution.py:429
  383.4 7.3 reduce-scatter.15.cloned.1.call-done
  393.0 43.4 %reduce-scatter.13.cloned.1.call-done = bf16[2,256,3,512]{3,1,2,0:T(8,128)(2,1)} async-done(((bf16[2,512,3,512]{3,1,2,0:T(8,128)(2,1)}), bf16[2,256,3,512]{3,1,2,0:T(8,128)(2,1)}) %reduce-scatter.13.cloned.1.call-update) | async-done | bytes 1572880 | tf_op jit(solution)/shard_map/reduce_scatter | solution.py:484
  442.9 50.8 %reduce-scatter.21.cloned.1.call-done = bf16[2,256,2048]{2,1,0:T(8,128)(2,1)} async-done(((bf16[2,512,2048]{2,1,0:T(8,128)(2,1)}), bf16[2,256,2048]{2,1,0:T(8,128)(2,1)}) %reduce-scatter.21.cloned.1.call-update) | async-done | bytes 2097168 | tf_op jit(solution)/shard_map/reduce_scatter | solution.py:484
  493.8 57.1 %reduce-scatter.17.cloned.1.call-done = bf16[2,256,2048]{2,1,0:T(8,128)(2,1)} async-done(((bf16[2,512,2048]{2,1,0:T(8,128)(2,1)}), bf16[2,256,2048]{2,1,0:T(8,128)(2,1)}) %reduce-scatter.17.cloned.1.call-update) | async-done | bytes 2097168 | tf_op jit(solution)/shard_map/reduce_scatter | solution.py:484
  559.3 16.2 %reduce-scatter.27.cloned.1.call-done = bf16[128,512]{1,0:T(8,128)(2,1)} async-done(((bf16[512,512]{1,0:T(8,128)(2,1)}), bf16[128,512]{1,0:T(8,128)(2,1)}) %reduce-scatter.27.cloned.1.call-update) | async-done | bytes 131088
  577.3 28.8 %reduce-scatter.25.cloned.1.call-done = bf16[128,1536]{1,0:T(8,128)(2,1)} async-done(((bf16[512,1536]{1,0:T(8,128)(2,1)}), bf16[128,1536]{1,0:T(8,128)(2,1)}) %reduce-scatter.25.cloned.1.call-update) | async-done | bytes 393232
  608.8 31.0 %reduce-scatter.23.cloned.1.call-done = bf16[2,256,512]{2,1,0:T(8,128)(2,1)} async-done(((bf16[2,256,2048]{2,1,0:T(8,128)(2,1)}), bf16[2,256,512]{2,1,0:T(8,128)(2,1)}) %reduce-scatter.23.cloned.1.call-update) | async-done | bytes 524304 | tf_op jit(solution)/shard_map/reduce_scatter | solution.py:485
  639.7 33.6 %reduce-scatter.19.cloned.1.call-done = bf16[2,256,512]{2,1,0:T(8,128)(2,1)} async-done(((bf16[2,256,2048]{2,1,0:T(8,128)(2,1)}), bf16[2,256,512]{2,1,0:T(8,128)(2,1)}) %reduce-scatter.19.cloned.1.call-update) | async-done | bytes 524304 | tf_op jit(solution)/shard_map/reduce_scatter | solution.py:485
  673.4 130.7 %all-reduce.10.cloned.1.call-done = (f32[2,6,512]{2,1,0:T(8,128)}, f32[2,3,512]{2,1,0:T(4,128)}, f32[2,169,16]{1,2,0:T(8,128)}, f32[2,2048]{1,0:T(2,128)}) async-done(((f32[2,6,512]{2,1,0:T(8,128)}, f32[2,3,512]{2,1,0:T(4,128)}, f32[2,169,16]{1,2,0:T(8,128)}, f32[2,2048]{1,0:T(2,128)}), (f32[2,6,512]{2,1,0:T(8,128)}, f32[2,3,512]{2,1,0:T(4,128)}, f32[2,169,16]{1,2,0:T(8,128)}, ...) | async-done | bytes 74896 | tf_op jit(solution)/shard_map/psum | solution.py:496
  812.6 18.9 %all-gather.25.cloned.1.call-done = bf16[4,588,512]{2,1,0:T(8,128)(2,1)} async-done(((bf16[1,588,512]{2,1,0:T(8,128)(2,1)}), bf16[4,588,512]{2,1,0:T(8,128)(2,1)}) %all-gather.25.cloned.1.call-update) | async-done | bytes 2408464 | tf_op jit(solution)/shard_map/all_gather | solution.py:481
  835.3 22.7 %all-gather.23.cloned.1.call-done = bf16[4,588,512]{2,1,0:T(8,128)(2,1)} async-done(((bf16[1,588,512]{2,1,0:T(8,128)(2,1)}), bf16[4,588,512]{2,1,0:T(8,128)(2,1)}) %all-gather.23.cloned.1.call-update) | async-done | bytes 2408464 | tf_op jit(solution)/shard_map/all_gather | solution.py:481
  861.7 69.0 %all-reduce.12.cloned.1.call-done = (bf16[2,256,3,128]{3,1,2,0:T(8,128)(2,1)}, bf16[2,256,128]{2,1,0:T(8,128)(2,1)}, bf16[2,256,512]{2,1,0:T(8,128)(2,1)}, bf16[2,256,512]{2,1,0:T(8,128)(2,1)}) async-done(((bf16[2,256,3,128]{3,1,2,0:T(8,128)(2,1)}, bf16[2,256,128]{2,1,0:T(8,128)(2,1)}, bf16[2,256,512]{2,1,0:T(8,128)(2,1)}, bf16[2,256,512]{2,1,0:T(8,128)(2,1)}), (bf16[2,256,3,128]{3,1,2,0:T(8,128)(2,1)}, ...) | async-done | bytes 1572880 | tf_op jit(solution)/shard_map/psum | solution.py:486
  (203 shorter events, 113.0 us)
Async XLA Ops:
  7.2 33.3 %all-gather.15.cloned.1.call-start = ((), (), s32[]{:S(2)}) async-start(), calls=%async_computation.10 | async-start | bytes 1572864 | tf_op jit(solution)/shard_map/all_gather | solution.py:455
  7.9 56.9 %all-gather.19.cloned.1.call-start = ((), (), s32[]{:S(2)}) async-start(), calls=%async_computation.12 | async-start | bytes 1572864 | tf_op jit(solution)/shard_map/all_gather | solution.py:455
  8.7 84.9 %all-gather.13.cloned.1.call-start = ((), (), s32[]{:S(2)}) async-start(), calls=%async_computation.9 | async-start | bytes 1310720 | tf_op jit(solution)/shard_map/all_gather | solution.py:455
  17.8 47.2 %copy-start.30 = (s32[49,49]{1,0:T(8,128)S(1)}, s32[49,49]{1,0:T(8,128)}, u32[]{:S(2)}) copy-start(s32[49,49]{1,0:T(8,128)} %param.20) | copy-start | bytes 28816
  17.8 47.3 %copy-start.33 = (f32[2,169,4]{1,2,0:T(4,128)S(1)}, f32[2,169,4]{1,2,0:T(4,128)}, u32[]{:S(2)}) copy-start(f32[2,169,4]{1,2,0:T(4,128)} %param.25) | copy-start | bytes 16228
  17.8 95.8 %all-gather.11.cloned.1.call-start = ((), (), s32[]{:S(2)}) async-start(), calls=%async_computation.8 | async-start | bytes 3932160 | tf_op jit(solution)/shard_map/all_gather | solution.py:455
  38.0 111.5 %all-gather.17.cloned.1.call-start = ((), (), s32[]{:S(2)}) async-start(), calls=%async_computation.11 | async-start | bytes 5242880 | tf_op jit(solution)/shard_map/all_gather | solution.py:455
  40.5 144.9 %all-gather.21.cloned.1.call-start = ((), (), s32[]{:S(2)}) async-start(), calls=%async_computation.13 | async-start | bytes 5242880 | tf_op jit(solution)/shard_map/all_gather | solution.py:455
  64.9 325.8 %reduce-scatter.15.cloned.1.call-start = ((), (), s32[]{:S(2)}) async-start(), calls=%async_computation.15 | async-start | bytes 1572864 | tf_op jit(solution)/shard_map/reduce_scatter | solution.py:484
  77.1 14.3 %copy-start.31 = (f32[2,512]{1,0:T(2,128)S(1)}, f32[2,512]{1,0:T(2,128)}, u32[]{:S(2)}) copy-start(f32[2,512]{1,0:T(2,128)} %sg.1) | copy-start | bytes 12292
  77.1 14.3 %copy-start.32 = (f32[2,512]{1,0:T(2,128)S(1)}, f32[2,512]{1,0:T(2,128)}, u32[]{:S(2)}) copy-start(f32[2,512]{1,0:T(2,128)} %fg.1) | copy-start | bytes 12292
  370.1 66.2 %reduce-scatter.13.cloned.1.call-start = ((), (), s32[]{:S(2)}) async-start(), calls=%async_computation.14 | async-start | bytes 4718592 | tf_op jit(solution)/shard_map/reduce_scatter | solution.py:484
  372.2 121.5 %reduce-scatter.21.cloned.1.call-start = ((), (), s32[]{:S(2)}) async-start(), calls=%async_computation.18 | async-start | bytes 6291456 | tf_op jit(solution)/shard_map/reduce_scatter | solution.py:484
  377.7 173.1 %reduce-scatter.17.cloned.1.call-start = ((), (), s32[]{:S(2)}) async-start(), calls=%async_computation.16 | async-start | bytes 6291456 | tf_op jit(solution)/shard_map/reduce_scatter | solution.py:484
  383.3 192.2 %reduce-scatter.27.cloned.1.call-start = ((), (), s32[]{:S(2)}) async-start(), calls=%async_computation.23 | async-start | bytes 655360
  393.0 213.0 %reduce-scatter.25.cloned.1.call-start = ((), (), s32[]{:S(2)}) async-start(), calls=%async_computation.22 | async-start | bytes 1966080
  442.8 196.9 %reduce-scatter.23.cloned.1.call-start = ((), (), s32[]{:S(2)}) async-start(), calls=%async_computation.19 | async-start | bytes 2621440 | tf_op jit(solution)/shard_map/reduce_scatter | solution.py:485
  493.7 57.2 %copy-start.21 = (f32[1,4,64,256]{3,2,1,0:T(8,128)S(1)}, f32[1,4,64,256]{3,2,1,0:T(8,128)}, u32[]{:S(2)}) copy-start(f32[1,4,64,256]{3,2,1,0:T(8,128)} %get-tuple-element.72) | copy-start | bytes 786436
  493.7 57.2 %copy-start.22 = (f32[1,4,64,256]{3,2,1,0:T(8,128)S(1)}, f32[1,4,64,256]{3,2,1,0:T(8,128)}, u32[]{:S(2)}) copy-start(f32[1,4,64,256]{3,2,1,0:T(8,128)} %get-tuple-element.71) | copy-start | bytes 786436
  493.7 179.6 %reduce-scatter.19.cloned.1.call-start = ((), (), s32[]{:S(2)}) async-start(), calls=%async_computation.17 | async-start | bytes 2621440 | tf_op jit(solution)/shard_map/reduce_scatter | solution.py:485
  550.9 253.2 %all-reduce.10.cloned.1.call-start = ((), (), s32[]{:S(2)}) async-start(), calls=%async_computation.24 | async-start | bytes 196608 | tf_op jit(solution)/shard_map/psum | solution.py:496
  556.0 275.5 %all-gather.25.cloned.1.call-start = ((), (), s32[]{:S(2)}) async-start(), calls=%async_computation.21 | async-start | bytes 3031040 | tf_op jit(solution)/shard_map/all_gather | solution.py:481
  558.3 299.7 %all-gather.23.cloned.1.call-start = ((), (), s32[]{:S(2)}) async-start(), calls=%async_computation.20 | async-start | bytes 3031040 | tf_op jit(solution)/shard_map/all_gather | solution.py:481
  559.3 371.4 %all-reduce.12.cloned.1.call-start = ((), (), s32[]{:S(2)}) async-start(), calls=%async_computation.25 | async-start | bytes 3145728 | tf_op jit(solution)/shard_map/psum | solution.py:486
  (31 other events, 83.7 us)
Sparse Core Ops, SparseCore 0:
  9.5 30.8 all-gather.14
  42.0 22.7 all-gather.18
  66.4 16.8 all-gather.12
  84.7 28.8 all-gather.10
  115.0 34.4 all-gather.16
  150.9 34.4 all-gather.20
  370.3 20.3 reduce-scatter.14
  392.9 43.3 reduce-scatter.12
  439.3 54.3 reduce-scatter.20
  496.4 54.3 reduce-scatter.16
  553.9 21.5 reduce-scatter.26
  577.9 28.0 reduce-scatter.24
  608.5 31.1 reduce-scatter.22
  642.1 31.1 reduce-scatter.18
  679.9 124.1 all-reduce.9
  806.1 25.4 all-gather.24
  833.5 24.4 all-gather.22
  861.6 69.0 all-reduce.11

commit v2 on v1

--- a/solution.py
+++ b/solution.py
@@ -1,5 +1,6 @@
 import functools
 import math
+import types
 
 import jax
 import jax.numpy as jnp
@@ -143,7 +144,7 @@
         normed, centered, inverse = norm_rows(hidden[at, :], gain, offset)
         low[at, :] = normed.astype(BF16)
         hat[at, :] = centered.astype(BF16)
-        inv[at, :] = inverse
+        inv[0][at, inv[1] : inv[1] + 1] = inverse
 
     loop(sz.pairs, body)
 
@@ -153,7 +154,7 @@
     for part in range(3):
 
         def body(i, part=part):
-            acc = mm(low[span(i, sz.chunk), :], weight[part]) + bias[part : part + 1, :]
+            acc = mm(low[span(i, sz.chunk), :], weight[part]) + bias[part]
             if part == 0:
                 acc = acc * HEAD ** (-0.5)
             for j in range(per):
@@ -202,7 +203,7 @@
     def body(i):
         rows = span(i // parts, sz.third)
         cols = span(lax.rem(i, parts), sz.width)
-        u = mm(low[rows, :], weight[:, cols]) + bias[:, cols]
+        u = mm(low[rows, :], weight[:, cols]) + bias(lax.rem(i, parts))
         phi = 0.5 + 0.5 * lax.erf(u * ROOT_HALF)
         act[rows, cols] = (u * phi).astype(BF16)
         slope[rows, cols] = (phi + u * (GAUSS * jnp.exp(-0.5 * u * u))).astype(BF16)
@@ -218,7 +219,7 @@
         weighted = up * gain
         first = jnp.mean(weighted, axis=-1, keepdims=True)
         second = jnp.mean(weighted * normed, axis=-1, keepdims=True)
-        grad[at, :] = grad[at, :] + inv[at, :] * (weighted - first - normed * second)
+        grad[at, :] = grad[at, :] + inv[0][at, inv[1] : inv[1] + 1] * (weighted - first - normed * second)
         sums[0] += fold(up * normed)
         sums[1] += fold(up)
 
@@ -298,7 +299,8 @@
                 halves[2].append(gather_heads(mm_tn(prob, grad), lane)[:ROWS])
             for part in range(3):
                 joined = jnp.concatenate(halves[part], axis=0)
-                outs[part, span(pair, 2 * ROWS), cols] = joined.astype(BF16)
+                at = slice(part * sz.width + group * LANES, part * sz.width + (group + 1) * LANES)
+                outs[span(pair, 2 * ROWS), at] = joined.astype(BF16)
                 totals[part, :, cols] += fold(joined)
 
     loop(sz.pairs, body)
@@ -344,162 +346,621 @@
     col = lax.broadcasted_iota(jnp.int32, (WIDE, LANES), 1) // HEAD
     return jnp.where(row == col, 1.0, 0.0).astype(BF16)
 
+
 def ones_mask():
     row = lax.broadcasted_iota(jnp.int32, (WIDE, WIDE), 0) // SLOT
     col = lax.broadcasted_iota(jnp.int32, (WIDE, WIDE), 1) // SLOT
     return jnp.where(row == col, 1.0, 0.0).astype(BF16)
 
-def forward_kernel(sz, x, wt, wp, we, wr, fg, fo, tb, pb, sg, so, eb, rb, bias, mask, heads, ones,
-                   out, n1, xh1, r1, q, k, v, probs, o64, oc, n2, xh2, r2, gp, act, ha, hb):
-    move = [image_to_window(sz.images, 0), window_to_window(sz.images, 0, SHIFT), window_to_image(sz.images, SHIFT)]
-    hb[...] = jnp.zeros_like(hb)
-    ha[...] = jnp.zeros_like(ha)
-    hb[0:592, :] = x[...].astype(F32)
-    move_rows(ha, hb, move[0])
-    bufs = [ha, hb]
-    for l in range(2):
-        h = bufs[l]
-        forward_norm(sz, h, fg[l:l+1, :], fo[l:l+1, :], n1.at[l], xh1.at[l], r1.at[l])
-        forward_triple(sz, n1.at[l], wt.at[l], tb.at[l], (q.at[l], k.at[l], v.at[l]))
-        forward_attend(sz, (q.at[l], k.at[l], v.at[l]), bias.at[l], mask if l else None, heads, ones, probs.at[l], o64.at[l], oc.at[l])
-        add_product(sz, h, oc.at[l], wp.at[l], pb[l:l+1, :])
-        forward_norm(sz, h, sg[l:l+1, :], so[l:l+1, :], n2.at[l], xh2.at[l], r2.at[l])
-        forward_expand(sz, n2.at[l], we.at[l], eb.at[l:l+1], act.at[l], gp.at[l])
-        add_product(sz, h, act.at[l], wr.at[l], rb[l:l+1, :])
-        if l == 0:
-            hb[...] = jnp.zeros_like(hb)
-            move_rows(hb, ha, move[1])
+
+MESH = pl.DeviceIdType.MESH
+KINDS = ("r", "e", "p", "t")
+LIMIT = 67_000_000
+PACK = 16
+SMALL = 32
+
+
+class Plan:
+    def __init__(self, sz, mine, ndp, nrow, ncol):
+        self.sz, self.mine, self.ndp, self.nrow, self.ncol = sz, mine, ndp, nrow, ncol
+        self.nj = ncol // 2
+        self.held = -(-mine // 16) * 16
+        self.deep = sz.width // nrow
+        self.thin = sz.width // ncol
+        self.broad = sz.hidden // ncol
+        self.offsets = [(a, b) for a in range(nrow) for b in range(self.nj) if (a, b) != (0, 0)]
+        self.nblocks = nrow * self.nj
+        self.spots = self.nblocks - 1
+
+    def block(self, kind, rows=None):
+        rows = self.deep if rows is None else rows
+        return {"t": (3, rows, self.thin), "p": (rows, self.thin)}.get(kind, (rows, self.broad))
+
+    def full(self, kind):
+        d, f = self.sz.width, self.sz.hidden
+        return {"t": (3, d, d), "p": (d, d)}.get(kind, (d, f))
+
+    def scratch(self):
+        sz = self.sz
+        T, D, F, W, G = sz.tokens, sz.width, sz.hidden, sz.windows, sz.groups
+        L = LAYERS
+        vm = pltpu.VMEM
+        dma = lambda *shape: pltpu.SemaphoreType.DMA(shape)
+        out = {}
+        for kind in KINDS:
+            out["w" + kind] = vm((L,) + self.full(kind), BF16)
+            out["g" + kind] = vm(self.full(kind), BF16)
+            out["h" + kind] = vm((L, self.nrow, self.nj) + self.block(kind), BF16)
+            out["x" + kind] = vm((L, self.spots) + self.block(kind), BF16)
+            out["z" + kind] = vm((L, self.ndp - 1) + self.block(kind, self.deep // self.ndp), BF16)
+        out.update(
+            nat_x=vm((self.held, D), BF16),
+            packs=vm((self.ncol, L, PACK, 512), F32),
+            table=vm((256, WIDE), F32),
+            index=vm((SLOT, WIDE), jnp.int32),
+            bias=vm((L, G, SLOT, WIDE), F32),
+            heads=vm((WIDE, LANES), BF16),
+            ones=vm((WIDE, WIDE), BF16),
+            ha=vm((T, D), F32),
+            hb=vm((T, D), F32),
+            n1=vm((L, T, D), BF16),
+            c1=vm((L, T, D), BF16),
+            n2=vm((L, T, D), BF16),
+            c2=vm((L, T, D), BF16),
+            inv=vm((T, LANES), F32),
+            q=vm((L, W, SLOT, D), BF16),
+            k=vm((L, W, SLOT, D), BF16),
+            v=vm((L, W, SLOT, D), BF16),
+            probs=vm((L, W, G, SLOT, WIDE), BF16),
+            slots=vm((L, W, SLOT, D), BF16),
+            rows=vm((T, D), BF16),
+            act=vm((T, F), BF16),
+            slope=vm((T, F), BF16),
+            low=vm((T, D), BF16),
+            pre=vm((T, F), BF16),
+            dslots=vm((W, SLOT, D), BF16),
+            ssum=vm((L, G, SLOT, WIDE), F32),
+            sums=vm((L, 6, 8, D), F32),
+            wide=vm((L, 8, F), F32),
+            tsum=vm((L, 3, 8, D), F32),
+            sm=vm((L, SMALL, 512), F32),
+            sm_pair=vm((L, SMALL, 512), F32),
+            sm_plane=vm((self.nblocks, L, SMALL, 512), F32),
+            sm_line=vm((self.ndp, L, SMALL, 512), F32),
+            in_sem=dma(4),
+            own_sem=dma(8),
+            far_send=dma(8, self.spots),
+            far_recv=dma(8, self.spots),
+            near_send=dma(8, self.nblocks),
+            near_recv=dma(8, self.nblocks),
+            pack_send=dma(self.ncol),
+            pack_recv=dma(self.ncol),
+            half_send=dma(8, self.nblocks),
+            half_recv=dma(8, self.nblocks),
+            plane_send=dma(8, self.spots),
+            plane_recv=dma(8, self.spots),
+            line_send=dma(8, self.ndp),
+            line_recv=dma(8, self.ndp),
+            last_send=dma(8, self.ndp),
+            last_recv=dma(8, self.ndp),
+            last_own=dma(8),
+            row_send=dma(2, 2 * self.nj),
+            row_recv=dma(2, 2 * self.nj),
+            row_own=dma(2),
+            sm_send=dma(3, self.nblocks + self.ndp),
+            sm_recv=dma(3, self.nblocks + self.ndp),
+            spill=dma(4),
+        )
+        return out
+
+
+def mega(plan, scale, names, *refs):
+    sz = plan.sz
+    inputs = ("tokens", "cot", "t_in", "p_in", "e_in", "r_in", "pack", "rel", "mask", "fg", "fo", "pb", "sg", "so", "rb")
+    outputs = ("out_h", "out_g", "o_t", "o_p", "o_e", "o_r", "small", "spill_a", "spill_s")
+    every = dict(zip(inputs + outputs + tuple(names), refs))
+    R = types.SimpleNamespace(**every)
+    for letter in "wghxz":
+        setattr(R, letter, {kind: every[letter + kind] for kind in KINDS})
+    R.i = {kind: every[kind + "_in"] for kind in KINDS}
+    R.o = {kind: every["o_" + kind] for kind in KINDS}
+    d, r, c = lax.axis_index("dp"), lax.axis_index("row"), lax.axis_index("col")
+    kk, j = lax.rem(c, 2), c // 2
+    T, D, F = sz.tokens, sz.width, sz.hidden
+    nr, nj, ndp = plan.nrow, plan.nj, plan.ndp
+    partner = (d, r, c + 1 - 2 * kk)
+
+    def plane(offset):
+        return (d, lax.rem(r + offset[0], nr), lax.rem(j + offset[1], nj) * 2 + kk)
+
+    def source(offset):
+        return lax.rem(r + nr - offset[0], nr), lax.rem(j + nj - offset[1], nj)
+
+    def remote(src, dst, send, recv, device):
+        return pltpu.make_async_remote_copy(
+            src_ref=src, dst_ref=dst, send_sem=send, recv_sem=recv, device_id=device, device_id_type=MESH
+        )
+
+    def cut(ref, kind, row, col):
+        rows = pl.ds(pl.multiple_of(row * plan.deep, plan.deep), plan.deep)
+        width = plan.thin if kind in "tp" else plan.broad
+        cols = pl.ds(pl.multiple_of(col * width, width), width)
+        return ref.at[:, rows, cols] if kind == "t" else ref.at[rows, cols]
+
+    peers = [(d, r, lax.rem(c + o, plan.ncol)) for o in range(1, plan.ncol)]
+    peers += [plane(o) for o in plan.offsets if o[0]]
+    peers += [(lax.rem(d + o, ndp), r, c) for o in range(1, ndp)]
+    barrier = pltpu.get_barrier_semaphore()
+    for peer in peers:
+        pl.semaphore_signal(barrier, inc=1, device_id=peer, device_id_type=MESH)
+
+    start = c * plan.mine
+    spare = lax.rem(start, 8)
+    rows_in = pl.ds(pl.multiple_of(start - spare, 8), plan.held)
+    in_x = pltpu.make_async_copy(R.tokens.at[rows_in, :], R.nat_x, R.in_sem.at[0])
+    in_c = pltpu.make_async_copy(R.cot.at[rows_in, :], R.low.at[0 : plan.held, :], R.in_sem.at[1])
+    in_x.start()
+    in_c.start()
+    order_of = [(layer, kind) for layer in range(LAYERS) for kind in "tper"]
+    own_copies = []
+    for s, (layer, kind) in enumerate(order_of):
+        copy = pltpu.make_async_copy(
+            R.i[kind].at[layer], cut(R.w[kind].at[layer], kind, r, c), R.own_sem.at[s]
+        )
+        copy.start()
+        own_copies.append(copy)
+    R.packs[c] = R.pack[...]
+
+    pl.semaphore_wait(barrier, len(peers))
+
+    pack_copies = []
+    for o in range(1, plan.ncol):
+        peer = (d, r, lax.rem(c + o, plan.ncol))
+        copy = remote(R.pack, R.packs.at[c], R.pack_send.at[o], R.pack_recv.at[o], peer)
+        copy.start()
+        pack_copies.append((o, copy))
+    far_copies, near_copies = [], []
+    for s, (layer, kind) in enumerate(order_of):
+        own = R.i[kind].at[layer]
+        here = cut(R.w[kind].at[layer], kind, r, c)
+        for i, offset in enumerate(plan.offsets):
+            copy = remote(own, here, R.far_send.at[s, i], R.far_recv.at[s, i], plane(offset))
+            copy.start()
+            far_copies.append(copy)
+        copy = remote(own, here, R.near_send.at[s, plan.spots], R.near_recv.at[s, plan.spots], partner)
+        copy.start()
+        near_copies.append(copy)
+
+    def weights_ready(s):
+        layer, kind = order_of[s]
+        whole = R.w[kind].at[layer]
+        for i, offset in enumerate(plan.offsets):
+            row, col = source(offset)
+            here = cut(whole, kind, row, col * 2 + kk)
+            remote(here, here, R.far_send.at[s, i], R.far_recv.at[s, i], partner).wait_recv()
+            copy = remote(here, here, R.near_send.at[s, i], R.near_recv.at[s, i], partner)
+            copy.start()
+            near_copies.append(copy)
+        own_copies[s].wait()
+        for i, offset in enumerate(plan.offsets):
+            row, col = source(offset)
+            here = cut(whole, kind, row, col * 2 + 1 - kk)
+            remote(here, here, R.near_send.at[s, i], R.near_recv.at[s, i], partner).wait_recv()
+        here = cut(whole, kind, r, c + 1 - 2 * kk)
+        remote(here, here, R.near_send.at[s, plan.spots], R.near_recv.at[s, plan.spots], partner).wait_recv()
+
+    R.heads[...] = head_mask()
+    R.ones[...] = ones_mask()
+    R.index[...] = jnp.full((SLOT, WIDE), -1, jnp.int32)
+    for h in range(GROUP):
+        R.index[0:CELLS, h * SLOT : h * SLOT + CELLS] = R.rel[...]
+    R.ha[...] = jnp.zeros((T, D), F32)
+    R.hb[...] = jnp.zeros((T, D), F32)
+    lane = lax.broadcasted_iota(jnp.int32, (SLOT, LANES), 1)
+
+    def load_rows(natural, wide, target, shift):
+        loop(plan.held // 16, lambda i: put(wide, i, natural))
+        for gap in sorted({col * plan.mine % 8 for col in range(plan.ncol)}):
+
+            @pl.when(spare == gap)
+            def _():
+                move_rows(target, wide, [(to, gap + at, n) for to, at, n in image_to_window(sz.images, shift)])
+
+    def put(wide, i, natural):
+        at = span(i, 16)
+        wide[at, :] = natural[at, :].astype(F32)
+
+    in_x.wait()
+    load_rows(R.nat_x, R.hb, R.ha, 0)
+
+    for o, _ in pack_copies:
+        from_col = lax.rem(c + plan.ncol - o, plan.ncol)
+        remote(R.pack, R.packs.at[from_col], R.pack_send.at[o], R.pack_recv.at[o], partner).wait_recv()
+    spread_row = lax.broadcasted_iota(jnp.int32, (8, WIDE), 0)
+    spread_col = lax.broadcasted_iota(jnp.int32, (8, WIDE), 1) // SLOT
+    spread_heads = jnp.where(spread_row == spread_col, 1.0, 0.0).astype(BF16)
+    key_lane = lax.rem(lax.broadcasted_iota(jnp.int32, (SLOT, WIDE), 1), SLOT)
+    empty = jnp.where(key_lane >= CELLS, GONE, 0.0)
+
+    def split(values):
+        high = values.astype(BF16)
+        rest = values - high.astype(F32)
+        middle = rest.astype(BF16)
+        return high, middle, (rest - middle.astype(F32)).astype(BF16)
+
+    def make_bias(layer):
+        for group in range(sz.groups):
+            heads_in = R.packs[group, layer, 4:12, 0:256]
+            R.table[...] = sum(mm_tn(part, spread_heads) for part in split(heads_in))
+
+            def step(i, acc):
+                for n in range(13):
+                    m = i * 13 + n
+                    acc = jnp.where(R.index[...] == m, R.table[pl.ds(m, 1), :], acc)
+                return acc
+
+            R.bias[layer, group] = lax.fori_loop(0, RELS // 13, step, empty)
+
+    def lanes_of(ref_of, count):
+        return jnp.concatenate([ref_of(g) for g in range(count)], axis=1)
+
+    make_bias(0)
+
+    for layer in range(LAYERS):
+        h = R.ha if layer == 0 else R.hb
+        base = 4 * layer
+        row1 = slice(layer, layer + 1)
+        forward_norm(sz, h, R.fg[row1, :], R.fo[row1, :], R.n1.at[layer], R.c1.at[layer], (R.inv, 2 * layer))
+        weights_ready(base)
+        bias3 = [lanes_of(lambda g, part=part: R.packs[g, layer, part : part + 1, 0:LANES], sz.groups) for part in range(3)]
+        forward_triple(sz, R.n1.at[layer], R.w["t"].at[layer], bias3, [ref.at[layer] for ref in (R.q, R.k, R.v)])
+        forward_attend(
+            sz, [ref.at[layer] for ref in (R.q, R.k, R.v)], R.bias.at[layer], R.mask if layer else None, R.heads, R.ones,
+            R.probs.at[layer], R.slots.at[layer], R.rows,
+        )
+        weights_ready(base + 1)
+        add_product(sz, h, R.rows, R.w["p"].at[layer], R.pb[row1, :])
+        forward_norm(sz, h, R.sg[row1, :], R.so[row1, :], R.n2.at[layer], R.c2.at[layer], (R.inv, 2 * layer + 1))
+        weights_ready(base + 2)
+        if layer:
+            for copy in spills:
+                copy.wait()
+        forward_expand(sz, R.n2.at[layer], R.w["e"].at[layer], lambda n: R.packs[n, layer, 3:4, :], R.act, R.slope)
+        if layer == 0:
+            spills = [
+                pltpu.make_async_copy(R.act, R.spill_a, R.spill.at[0]),
+                pltpu.make_async_copy(R.slope, R.spill_s, R.spill.at[1]),
+            ]
+            for copy in spills:
+                copy.start()
+            make_bias(1)
+        weights_ready(base + 3)
+        add_product(sz, h, R.act, R.w["r"].at[layer], R.rb[row1, :])
+        if layer == 0:
+            R.hb[...] = jnp.zeros((T, D), F32)
+            move_rows(R.hb, R.ha, window_to_window(sz.images, 0, SHIFT))
+
+    def send_rows(which, natural, wide, out):
+        def narrow(i):
+            at = span(i, 16)
+            natural[at, :] = wide[at, :].astype(BF16)
+
+        loop(plan.held // 16, narrow)
+        own = pltpu.make_async_copy(natural, out.at[c], R.row_own.at[which])
+        own.start()
+        copies = []
+        for b in range(1, nj):
+            copies.append(remote(natural, out.at[c], R.row_send.at[which, b], R.row_recv.at[which, b], plane((0, b))))
+        copies.append(remote(natural, out.at[c], R.row_send.at[which, 0], R.row_recv.at[which, 0], partner))
+        for copy in copies:
+            copy.start()
+        return own, copies
+
+    def relay_rows(which, natural, out):
+        copies = []
+        for b in range(1, nj):
+            at = out.at[lax.rem(j + nj - b, nj) * 2 + kk]
+            remote(natural, at, R.row_send.at[which, b], R.row_recv.at[which, b], partner).wait_recv()
+            copy = remote(at, at, R.row_send.at[which, nj + b], R.row_recv.at[which, nj + b], partner)
+            copy.start()
+            copies.append(copy)
+        return copies
+
+    def finish_rows(which, natural, out, own, copies):
+        own.wait()
+        for copy in copies:
+            copy.wait_send()
+        at = out.at[c + 1 - 2 * kk]
+        remote(natural, at, R.row_send.at[which, 0], R.row_recv.at[which, 0], partner).wait_recv()
+        for b in range(1, nj):
+            at = out.at[lax.rem(j + nj - b, nj) * 2 + 1 - kk]
+            remote(natural, at, R.row_send.at[which, nj + b], R.row_recv.at[which, nj + b], partner).wait_recv()
+
+    move_rows(R.ha, R.hb, window_to_image(sz.images, SHIFT))
+    own_h, sent_h = send_rows(0, R.nat_x, R.ha, R.out_h)
+    for copy in far_copies + near_copies:
+        copy.wait_send()
+    for _, copy in pack_copies:
+        copy.wait_send()
+
+    pending = []
+
+    def stage_half(kind, layer):
+        n = KINDS.index(kind) * 2 + layer
+        for a in range(nr):
+            for b in range(nj):
+                i = a * nj + b
+                copy = remote(
+                    cut(R.g[kind], kind, a, 2 * b + 1 - kk), R.h[kind].at[layer, a, b],
+                    R.half_send.at[n, i], R.half_recv.at[n, i], partner,
+                )
+                copy.start()
+
+    def stage_plane(kind, layer):
+        n = KINDS.index(kind) * 2 + layer
+        for a in range(nr):
+            for b in range(nj):
+                i = a * nj + b
+                copy = remote(
+                    cut(R.g[kind], kind, a, 2 * b + 1 - kk), R.h[kind].at[layer, a, b],
+                    R.half_send.at[n, i], R.half_recv.at[n, i], partner,
+                )
+                copy.wait()
+                add_blocks(plan, kind, R.h[kind].at[layer, a, b], [cut(R.g[kind], kind, a, 2 * b + kk)])
+        for i, offset in enumerate(plan.offsets):
+            row, col = lax.rem(r + offset[0], nr), lax.rem(j + offset[1], nj)
+            copy = remote(
+                R.h[kind].at[layer, row, col], R.x[kind].at[layer, i],
+                R.plane_send.at[n, i], R.plane_recv.at[n, i], plane(offset),
+            )
+            copy.start()
+            pending.append(copy)
+
+    step_rows = plan.deep // ndp
+
+    def part(ref, kind, index):
+        rows = pl.ds(pl.multiple_of(index * step_rows, step_rows), step_rows)
+        return ref.at[:, rows, :] if kind == "t" else ref.at[rows, :]
+
+    def stage_line(kind, layer):
+        n = KINDS.index(kind) * 2 + layer
+        own = R.h[kind].at[layer, r, j]
+        for i, offset in enumerate(plan.offsets):
+            there = R.x[kind].at[layer, i]
+            remote(there, there, R.plane_send.at[n, i], R.plane_recv.at[n, i], partner).wait_recv()
+        add_blocks(plan, kind, own, [R.x[kind].at[layer, i] for i in range(plan.spots)])
+        for o in range(1, ndp):
+            to = lax.rem(d + o, ndp)
+            copy = remote(
+                part(own, kind, to), R.z[kind].at[layer, o - 1], R.line_send.at[n, o], R.line_recv.at[n, o], (to, r, c)
+            )
+            copy.start()
+            pending.append(copy)
+
+    def stage_last(kind, layer):
+        n = KINDS.index(kind) * 2 + layer
+        own = part(R.h[kind].at[layer, r, j], kind, d)
+        for o in range(1, ndp):
+            there = R.z[kind].at[layer, o - 1]
+            remote(there, there, R.line_send.at[n, o], R.line_recv.at[n, o], partner).wait_recv()
+        add_blocks(plan, kind, own, [R.z[kind].at[layer, i] for i in range(ndp - 1)])
+        there = part(R.o[kind].at[layer], kind, d)
+        copy = pltpu.make_async_copy(own, there, R.last_own.at[n])
+        copy.start()
+        for o in range(1, ndp):
+            to = (lax.rem(d + o, ndp), r, c)
+            copy = remote(own, there, R.last_send.at[n, o], R.last_recv.at[n, o], to)
+            copy.start()
+            pending.append(copy)
+
+    def stage_end(kind, layer):
+        n = KINDS.index(kind) * 2 + layer
+        own = part(R.h[kind].at[layer, r, j], kind, d)
+        pltpu.make_async_copy(own, part(R.o[kind].at[layer], kind, d), R.last_own.at[n]).wait()
+        for o in range(1, ndp):
+            there = part(R.o[kind].at[layer], kind, lax.rem(d + ndp - o, ndp))
+            remote(own, there, R.last_send.at[n, o], R.last_recv.at[n, o], partner).wait_recv()
+
+    in_c.wait()
+    R.hb[...] = jnp.zeros((T, D), F32)
+    load_rows(R.low, R.ha, R.hb, SHIFT)
+    for layer in reversed(range(LAYERS)):
+        e, dn = (R.hb, R.ha) if layer else (R.ha, R.hb)
+        row1 = slice(layer, layer + 1)
+        inv1 = (R.inv, 2 * layer)
+        inv2 = (R.inv, 2 * layer + 1)
+        sums = R.sums.at[layer]
+        first = layer == LAYERS - 1
+        round_grad(sz, e, R.low, None, sums.at[0])
+        if not first:
+            for copy in fills:
+                copy.wait()
+        weight_grad(F // D, R.low, R.act, D, R.g["r"], scale)
+        stage_half("r", layer)
+        backward_hidden(sz, R.low, R.w["r"].at[layer], R.slope, R.pre, R.wide.at[layer])
+        if first:
+            fills = [
+                pltpu.make_async_copy(R.spill_a, R.act, R.spill.at[2]),
+                pltpu.make_async_copy(R.spill_s, R.slope, R.spill.at[3]),
+            ]
+            for copy in fills:
+                copy.start()
+            relayed_h = relay_rows(0, R.nat_x, R.out_h)
         else:
-            move_rows(ha, hb, move[2])
-            out[...] = ha[0:592, :]
-
-def backward_kernel(sz, scale, which, cot, wt, wp, we, wr, fg, sg, heads, n1, xh1, r1, q, k, v, probs, o64, oc, n2, xh2, r2, gp, act,
-                    out, gt, gp_, ge, gr, small, big, tsum, ssum, ga, gb, low, pre, dn, do64, dc, sums):
-    move = [image_to_window(sz.images, SHIFT), window_to_window(sz.images, SHIFT, 0), window_to_image(sz.images, 0)]
-    ga[...] = jnp.zeros_like(ga); gb[...] = jnp.zeros_like(gb)
-    if which:
-        ga[0:592, :] = cot[...].astype(F32)
-        move_rows(gb, ga, move[0])
-    else:
-        gb[...] = cot[...]
-    lane = lax.broadcasted_iota(jnp.int32, (SLOT, LANES), 1)
-    l = 0
-    e = gb
-    round_grad(sz, e, low, None, small.at[l, 0])
-    weight_grad(4, low, act.at[l], sz.width, gr.at[l], scale)
-    backward_hidden(sz, low, wr.at[l], gp.at[l], pre, big.at[l])
-    weight_grad(4, n2.at[l], pre, sz.width, ge.at[l], scale)
-    back_product(sz, [pre], [we.at[l]], dn)
-    backward_norm(sz, dn, e, xh2.at[l], r2.at[l], sg[l:l+1, :], small.at[l, 1:3])
-    round_grad(sz, e, low, None, small.at[l, 3])
-    weight_grad(1, low, oc.at[l], sz.width, gp_.at[l], scale)
-    backward_out(sz, low, wp.at[l], do64)
-    backward_attend(sz, (q.at[l], k.at[l], v.at[l]), probs.at[l], o64.at[l], do64, heads, lane, dc, tsum.at[l], ssum.at[l])
-    for part in range(3):
-        weight_grad(1, n1.at[l], dc.at[part], sz.width, gt.at[l, part], scale)
-    back_product(sz, [dc.at[p] for p in range(3)], [wt.at[l, p] for p in range(3)], dn)
-    backward_norm(sz, dn, e, xh1.at[l], r1.at[l], fg[l:l+1, :], small.at[l, 4:6])
-    ga[...] = jnp.zeros_like(ga)
-    if which:
-        move_rows(ga, gb, move[1])
-        out[...] = ga[...]
-    else:
-        move_rows(ga, gb, move[2])
-        out[...] = ga[...]
-
-LIMIT = 66_900_000
-def saved_shapes(sz):
-    L, T, D, W = 2, sz.tokens, sz.width, sz.windows
-    return [((L,T,D),BF16),((L,T,D),BF16),((L,T,1),F32),((L,W,SLOT,D),BF16),((L,W,SLOT,D),BF16),((L,W,SLOT,D),BF16),
-            ((L,W,sz.groups,SLOT,WIDE),BF16),((L,W,SLOT,D),BF16),((L,T,D),BF16),((L,T,D),BF16),((L,T,D),BF16),((L,T,1),F32),
-            ((L,T,sz.hidden),BF16),((L,T,sz.hidden),BF16)]
-VM = pl.BlockSpec(memory_space=pltpu.VMEM)
-
-def fwd_call(sz, *args):
-    shapes = [((592, sz.width), F32)] + saved_shapes(sz)
-    return pl.pallas_call(functools.partial(forward_kernel, sz),
-        out_shape=[jax.ShapeDtypeStruct(s, d) for s, d in shapes],
-        in_specs=[VM]*len(args), out_specs=[VM]*len(shapes),
-        scratch_shapes=[pltpu.VMEM((sz.tokens, sz.width), F32)]*2,
-        compiler_params=pltpu.CompilerParams(vmem_limit_bytes=LIMIT), name="fwd")(*args)
-
-def bwd_one(sz, scale, which, *args):
-    L,D,T,F = 1, sz.width, sz.tokens, sz.hidden
-    shapes = [((T,D),F32), ((L,3,D,D),BF16), ((L,D,D),BF16), ((L,D,F),BF16), ((L,D,F),BF16), ((L,6,8,D),F32), ((L,8,F),F32), ((L,3,8,D),F32), ((L,sz.groups,SLOT,WIDE),F32)]
-    return pl.pallas_call(functools.partial(backward_kernel, sz, scale, which),
-        out_shape=[jax.ShapeDtypeStruct(s, d) for s, d in shapes],
-        in_specs=[VM]*len(args), out_specs=[VM]*len(shapes),
-        scratch_shapes=[pltpu.VMEM((T,D),F32)]*2+[pltpu.VMEM((T,D),BF16), pltpu.VMEM((T,F),BF16), pltpu.VMEM((T,D),F32), pltpu.VMEM((sz.windows,SLOT,D),BF16), pltpu.VMEM((3,T,D),BF16), pltpu.VMEM((8,128),F32)],
-        compiler_params=pltpu.CompilerParams(vmem_limit_bytes=LIMIT), name="bwd%d"%which)(*args)
-
-def bwd_call(sz, scale, cot, *args):
-    one = lambda which, c: bwd_one(sz, scale, which, c, *[a if a.shape[0] != 2 else a[which:which+1] for a in args])
-    b = one(1, cot)
-    c = one(0, b[0])
-    return [c[0][:592]] + [jnp.concatenate([x, y], 0) for x, y in zip(c[1:], b[1:])]
+            stage_line("t", 1)
+        weight_grad(F // D, R.n2.at[layer], R.pre, D, R.g["e"], scale)
+        stage_half("e", layer)
+        stage_plane("r", layer)
+        back_product(sz, [R.pre], [R.w["e"].at[layer]], dn)
+        backward_norm(sz, dn, e, R.c2.at[layer], inv2, R.sg[row1, :], sums.at[1:3])
+        round_grad(sz, e, R.low, None, sums.at[3])
+        collect_rows(sz, R.slots.at[layer], R.rows)
+        weight_grad(1, R.low, R.rows, D, R.g["p"], scale)
+        stage_half("p", layer)
+        stage_plane("e", layer)
+        if not first:
+            stage_last("t", 1)
+        backward_out(sz, R.low, R.w["p"].at[layer], R.dslots)
+        stage_line("r", layer)
+        stage_plane("p", layer)
+        backward_attend(
+            sz, [ref.at[layer] for ref in (R.q, R.k, R.v)], R.probs.at[layer], R.slots.at[layer], R.dslots, R.heads, lane,
+            R.pre, R.tsum.at[layer], R.ssum.at[layer],
+        )
+        stage_line("e", layer)
+        stage_last("r", layer)
+        for piece in range(3):
+            cols = slice(piece * D, (piece + 1) * D)
+            weight_grad(1, R.n1.at[layer], R.pre.at[:, cols], D, R.g["t"].at[piece], scale)
+        stage_half("t", layer)
+        stage_line("p", layer)
+        back_product(
+            sz, [R.pre.at[:, p * D : (p + 1) * D] for p in range(3)], [R.w["t"].at[layer, p] for p in range(3)], dn
+        )
+        stage_plane("t", layer)
+        backward_norm(sz, dn, e, R.c1.at[layer], inv1, R.fg[row1, :], sums.at[4:6])
+        stage_last("e", layer)
+        stage_last("p", layer)
+        if layer:
+            R.ha[...] = jnp.zeros((T, D), F32)
+            move_rows(R.ha, R.hb, window_to_window(sz.images, SHIFT, 0))
+    move_rows(R.hb, R.ha, window_to_image(sz.images, 0))
+    finish_rows(0, R.nat_x, R.out_h, own_h, sent_h + relayed_h)
+    own_g, sent_g = send_rows(1, R.nat_x, R.hb, R.out_g)
+
+    R.sm[...] = jnp.zeros(R.sm.shape, F32)
+    for layer in range(LAYERS):
+        sm = R.sm.at[layer]
+        for row, at in enumerate((4, 5, None, None, None, 3, 1, 2, 0)):
+            if at is not None:
+                sm[row : row + 1, :] = jnp.sum(R.sums[layer, at], axis=0, keepdims=True) * scale
+        for p in range(3):
+            sm[2 + p : 3 + p, :] = jnp.sum(R.tsum[layer, p], axis=0, keepdims=True) * scale
+        for p in range(F // D):
+            cols = slice(p * D, (p + 1) * D)
+            sm[9 + p : 10 + p, :] = jnp.sum(R.wide[layer, :, cols], axis=0, keepdims=True) * scale
+
+    def table_grads(layer):
+        for group in range(sz.groups):
+            R.table[...] = jnp.zeros((256, WIDE), F32)
+
+            def step(i):
+                for n in range(13):
+                    m = i * 13 + n
+                    chosen = jnp.where(R.index[...] == m, R.ssum[layer, group], 0.0)
+                    R.table[pl.ds(m, 1), :] = jnp.sum(chosen, axis=0, keepdims=True)
+
+            loop(RELS // 13, step)
+            total = sum(mm_nt(spread_heads, p) for p in split(R.table[...]))
+            at = 16 + GROUP * group
+            R.sm[layer, at : at + GROUP, 0:256] = total[0:GROUP] * scale
+
+    table_grads(1)
+    stage_line("t", 0)
+    relayed_g = relay_rows(1, R.nat_x, R.out_g)
+    table_grads(0)
+    pair = remote(R.sm, R.sm_pair, R.sm_send.at[0, 0], R.sm_recv.at[0, 0], partner)
+    pair.start()
+    stage_last("t", 0)
+    pair.wait()
+    own = R.sm_plane.at[r * nj + j]
+    own[...] = R.sm[...] + R.sm_pair[...]
+    for i, offset in enumerate(plan.offsets):
+        copy = remote(own, own, R.sm_send.at[1, i], R.sm_recv.at[1, i], plane(offset))
+        copy.start()
+        pending.append(copy)
+    for i, offset in enumerate(plan.offsets):
+        row, col = source(offset)
+        there = R.sm_plane.at[row * nj + col]
+        remote(there, there, R.sm_send.at[1, i], R.sm_recv.at[1, i], partner).wait_recv()
+    own = R.sm_line.at[d]
+    own[...] = sum(R.sm_plane[i] for i in range(plan.nblocks))
+    for o in range(1, ndp):
+        to = (lax.rem(d + o, ndp), r, c)
+        copy = remote(own, own, R.sm_send.at[2, o], R.sm_recv.at[2, o], to)
+        copy.start()
+        pending.append(copy)
+    for o in range(1, ndp):
+        there = R.sm_line.at[lax.rem(d + ndp - o, ndp)]
+        remote(there, there, R.sm_send.at[2, o], R.sm_recv.at[2, o], partner).wait_recv()
+    R.small[...] = sum(R.sm_line[i] for i in range(ndp))
+    finish_rows(1, R.nat_x, R.out_g, own_g, sent_g + relayed_g)
+    for kind in KINDS:
+        for layer in range(LAYERS):
+            stage_end(kind, layer)
+    for copy in pending:
+        copy.wait_send()
+
+
+def add_blocks(plan, kind, into, others):
+    rows = into.shape[-2]
+    step = min(64, rows)
+    planes = range(into.shape[0]) if kind == "t" else (None,)
+    for p in planes:
+
+        def body(i, p=p):
+            at = (span(i, step), slice(None)) if p is None else (p, span(i, step), slice(None))
+            total = into[at].astype(F32)
+            for other in others:
+                total = total + other[at].astype(F32)
+            into[at] = total.astype(BF16)
+
+        loop(rows // step, body)
+
+
+def collect_rows(sz, slots, rows):
+    def body(pair):
+        halves = [slots[pair * 2 + half].astype(F32)[:ROWS] for half in range(2)]
+        rows[span(pair, 2 * ROWS), :] = jnp.concatenate(halves, axis=0).astype(BF16)
+
+    loop(sz.pairs, body)
 
 
 def shards(
     block_input, cotangent, region_ids, rel_index, first_gain, first_offset, triple_weight, triple_bias, rel_table,
     project_weight, project_bias, second_gain, second_offset, expand_weight, expand_bias, reduce_weight, reduce_bias,
 ):
-    cols = lax.axis_size("col")
+    ndp, nrow, ncol = (lax.axis_size(name) for name in ("dp", "row", "col"))
     tokens = block_input.shape[0]
-    mine = tokens // cols
-    scale = 1.0 / math.sqrt(tokens * lax.axis_size("dp") * lax.axis_size("row"))
-    sz = Sizes(mine // (SIDE * SIDE), block_input.shape[1], expand_weight.shape[2] * cols)
-    held = -(-mine // 16) * 16
-    start = lax.axis_index("col") * mine
-
-    def whole(weight, last):
-        return lax.all_gather(lax.all_gather(weight, "row", axis=1, tiled=True), "col", axis=last, tiled=True)
-
-    wt = jnp.transpose(whole(triple_weight, 3), (0, 2, 1, 3))
-    wp, we, wr = whole(project_weight, 2), whole(expand_weight, 2), whole(reduce_weight, 2)
-    tb = lax.all_gather(triple_bias, "col", axis=2, tiled=True)
-    eb = lax.all_gather(expand_bias, "col", axis=1, tiled=True)
-    table = lax.all_gather(rel_table, "col", axis=2, tiled=True)
-    cut = lambda rows: jnp.pad(lax.dynamic_slice_in_dim(rows, start, mine, 0), ((0, held - mine), (0, 0)))
-    onehot = rel_onehot(rel_index)
-    bias = jnp.stack([rel_bias(onehot, table[layer]) for layer in range(LAYERS)])
-    bias = jnp.pad(bias, ((0, 0), (0, 0), (0, SLOT - CELLS), (0, 0)))
-    bias = jnp.pad(bias, ((0, 0), (0, 0), (0, 0), (0, SLOT - CELLS)), constant_values=GONE)
-    bias = bias.reshape(LAYERS, sz.groups, GROUP, SLOT, SLOT).transpose(0, 1, 3, 2, 4)
-    bias = bias.reshape(LAYERS, sz.groups, SLOT, WIDE)
+    mine = tokens // ncol
+    scale = 1.0 / math.sqrt(tokens * ndp * nrow)
+    sz = Sizes(mine // (SIDE * SIDE), block_input.shape[1], expand_weight.shape[2] * ncol)
+    plan = Plan(sz, mine, ndp, nrow, ncol)
+    pad = lambda value: jnp.pad(value, ((0, 0), (0, 0), (0, 512 - value.shape[2])))
+    pack = jnp.concatenate(
+        [pad(triple_bias), pad(expand_bias[:, None]), pad(jnp.transpose(rel_table, (0, 2, 1))), jnp.zeros((LAYERS, 8, 512), F32)], axis=1
+    )
     mask = jnp.pad(region_mask(region_ids), ((0, 0), (0, SLOT - CELLS), (0, SLOT - CELLS)))
     mask = jnp.tile(mask, (1, 1, GROUP))
-    heads = head_mask()
-    saved = fwd_call(
-        sz, cut(block_input), wt, wp, we, wr, first_gain, first_offset, tb, project_bias, second_gain, second_offset, eb,
-        reduce_bias, bias, mask, heads, ones_mask(),
+    vmem = pl.BlockSpec(memory_space=pltpu.VMEM)
+    hbm = pl.BlockSpec(memory_space=pl.ANY)
+    scratch = plan.scratch()
+    D, T, F = sz.width, sz.tokens, sz.hidden
+    outs = [((ncol, plan.held, D), BF16)] * 2
+    outs += [((LAYERS,) + plan.block(kind), BF16) for kind in "tper"]
+    outs += [((LAYERS, SMALL, 512), F32), ((T, F), BF16), ((T, F), BF16)]
+    got = pl.pallas_call(
+        functools.partial(mega, plan, scale, tuple(scratch)),
+        out_shape=[jax.ShapeDtypeStruct(*o) for o in outs],
+        in_specs=[hbm] * 6 + [vmem] * 9,
+        out_specs=[hbm] * 6 + [vmem] + [hbm] * 2,
+        scratch_shapes=list(scratch.values()),
+        compiler_params=pltpu.CompilerParams(collective_id=0, has_side_effects=True, vmem_limit_bytes=LIMIT),
+        name="blocks",
+    )(
+        block_input, cotangent, jnp.transpose(triple_weight, (0, 2, 1, 3)), project_weight, expand_weight, reduce_weight, pack,
+        rel_index, mask, first_gain, first_offset, project_bias, second_gain, second_offset, reduce_bias,
     )
-    back = bwd_call(
-        sz, scale, cut(cotangent), wt, wp, we, wr, first_gain, second_gain, heads, *saved[1:]
-    )
-
-    def rows_out(rows):
-        return lax.all_gather(rows[:mine].astype(BF16), "col", axis=0, tiled=True).astype(F32)
-
-    def scatter(grad, last):
-        grad = lax.psum_scatter(grad, "row", scatter_dimension=1, tiled=True)
-        grad = lax.psum_scatter(grad, "col", scatter_dimension=last, tiled=True)
-        return lax.psum(grad, "dp").astype(F32)
-
-    gt = scatter(jnp.transpose(back[1], (0, 2, 1, 3)), 3)
-    gp, ge, gr = scatter(back[2], 2), scatter(back[3], 2), scatter(back[4], 2)
-    small = jnp.sum(back[5], axis=2) * scale
-    big = jnp.sum(back[6], axis=1) * scale
-    tsum = jnp.sum(back[7], axis=2) * scale
-    ssum = back[8].reshape(LAYERS, sz.groups, SLOT, GROUP, SLOT)[:, :, :CELLS, :, :CELLS]
-    ssum = ssum.transpose(0, 1, 3, 2, 4).reshape(LAYERS, sz.groups * GROUP, CELLS * CELLS)
-    gtab = jnp.einsum("lhp,pm->lmh", ssum, onehot, precision=lax.Precision.HIGHEST) * scale
-    small, big, tsum, gtab = lax.psum((small, big, tsum, gtab), ("dp", "row", "col"))
-    own = lambda value, axis: lax.dynamic_slice_in_dim(
-        value, lax.axis_index("col") * (value.shape[axis] // cols), value.shape[axis] // cols, axis
-    )
+    out_h, out_g, gt, gp, ge, gr, small = got[:7]
+    whole = lambda rows: rows[:, :mine].reshape(tokens, D).astype(F32)
+    col = lax.axis_index("col")
+    tri = lax.dynamic_slice_in_dim(small[:, 2:5], col * plan.thin, plan.thin, 2)
+    wide = lax.dynamic_slice_in_dim(small, 9 + col, 1, 1)[:, 0]
+    heads = lax.dynamic_slice_in_dim(small[:, 16:32, :RELS], col * (16 // ncol), 16 // ncol, 1)
     return (
-        rows_out(saved[0]), rows_out(back[0]), small[:, 4], small[:, 5], gt, own(tsum, 2), own(gtab, 2), gp, small[:, 3],
-        small[:, 1], small[:, 2], ge, own(big, 1), gr, small[:, 0],
+        whole(out_h), whole(out_g), small[:, 0], small[:, 1], jnp.transpose(gt, (0, 2, 1, 3)).astype(F32), tri,
+        jnp.transpose(heads, (0, 2, 1)), gp.astype(F32), small[:, 5], small[:, 6], small[:, 7], ge.astype(F32), wide,
+        gr.astype(F32), small[:, 8],
     )
 
 

time: 950 us -> 280 us (0.29)
  waiting for transfers between devices: 623 us -> 0 us
  Pallas kernels: 150 us -> 248 us
  local copies, waits for them, and re-layouts: 84 us -> 18 us
  blocking collectives: 45.6 us -> 0 us
  between operations: 15 us -> 0.72 us
    reduce_scatter x6 -> x0, waiting for transfers between devices: 223 us -> none  [the longest x4 159 us: scatter(): grad = lax.psum_scatter(grad, 'row', scatter_dimension=1, tiled=True)]
    psum x2 -> x0, waiting for transfers between devices: 200 us -> none  [the longest x1 131 us: shards(): lax.psum((small, big, tsum, gtab), ('dp', 'row', 'col'))]
    all_gather x8 -> x0, waiting for transfers between devices: 154 us -> none  [the longest x4 85.6 us: whole(): lax.all_gather(lax.all_gather(weight, 'row', axis=1, tiled=True), 'col',...]
    pallas_call x3 -> x1, Pallas kernels: 150 us -> 248 us  [shards(): pl.pallas_call(functools.partial(mega, plan, scale, tuple(scratch)), out_...]
    unnamed x20 -> x0, waiting for transfers between devices: 46.6 us -> none
    all_gather x5 -> x0, blocking collectives: 45.6 us -> none  [the longest x2 29.2 us: whole(): lax.all_gather(weight, 'row', axis=1, tiled=True)]
    slice x22 -> x3, local copies, waits for them, and re-layouts: 37 us -> 2.55 us  [the longest x1 1.03 us: shards(): small[:, 8]]
    unnamed x94 -> x14, local copies, waits for them, and re-layouts: 27.4 us -> 3.68 us
  transfers between devices with their start and end apart: 18 -> 0, of which waited for: 17 -> 0; matrix products, arithmetic and copies ran while one was open for 7% -> 0% of each run, Pallas kernels for 0% -> 0%
where the time goes in v2:
time: 280 us
  Pallas kernels  248 us (89%)
  local copies, waits for them, and re-layouts  18 us (6%)
  other arithmetic  12.9 us (5%)
    pallas_call x1, Pallas kernels, shards(): pl.pallas_call(functools.partial(mega, plan, scale, tuple(scratch)), out_...  248 us
    convert_element_type x2, local copies, waits for them, and re-layouts, shards(): whole = lambda rows: rows[:, :mine].reshape(tokens, D).astype(F32)  8.35 us
    convert_element_type x1, other arithmetic, shards(): whole = lambda rows: rows[:, :mine].reshape(tokens, D).astype(F32)  7.56 us

profile of v2, /device:TPU:0, one launch (start us, length us, event | category | flops | bytes accessed | tf_op | source)
XLA Modules:
  0.0 279.7 jit_solution(7190625778343989214)
XLA Ops:
  0.6 0.8 reshape_reshape_reshape.3
  1.5 0.1 compare_select_fusion
  1.7 0.1 tile.4
  1.8 1.0 tile.10.refs_8_
  2.8 0.7 broadcast_in_dim.14
  3.5 0.7 copy.34
  4.3 1.4 fusion.refs_6_
  5.7 248.0 %blocks.1 = (bf16[4,592,512]{2,1,0:T(8,128)(2,1)}, bf16[4,592,512]{2,1,0:T(8,128)(2,1)}, bf16[2,3,256,128]{3,2,1,0:T(8,128)(2,1)}, bf16[2,256,128]{2,1,0:T(8,128...) custom-call(bf16[2352,512]{1,0:T(8,128)(2,1)} %refs_0_.1, ...), custom_call_target="tpu_custom_call" | custom-call | tf_op jit(solution)/shard_map/blocks/pallas_call | solution.py:942
  253.7 1.0 fusion.2
  254.7 0.6 copy_bitcast_fusion
  255.3 0.6 copy_bitcast_fusion.2
  255.9 0.6 copy_bitcast_fusion.4
  256.5 0.6 copy.51
  257.1 0.8 slice.35
  257.9 0.6 dynamic-slice_bitcast_fusion
  258.5 0.8 slice.34
  259.3 0.6 copy.36
  259.9 7.6 %slice_convert_fusion = (f32[4,588,512]{2,1,0:T(8,128)}, f32[4,588,512]{2,1,0:T(8,128)}) fusion(bf16[4,592,512]{2,1,0:T(8,128)(2,1)} %get-tuple-element.23, bf16[4,592,512]{2,1,0:T(8,128)(2,1)} %get-tuple-element.22), kind=kLoop, calls=%fused_computation | loop fusion | flops 2408448 | bytes 14450688 | tf_op jit(solution)/shard_map/convert_element_type | solution.py:955
  267.4 4.1 %reshape.42 = f32[2352,512]{1,0:T(8,128)} reshape(f32[4,588,512]{2,1,0:T(8,128)} %get-tuple-element.67) | data formatting | bytes 9633792 | tf_op jit(solution)/shard_map/convert_element_type | solution.py:955
  271.6 4.2 %reshape.43 = f32[2352,512]{1,0:T(8,128)} reshape(f32[4,588,512]{2,1,0:T(8,128)} %get-tuple-element.66) | data formatting | bytes 9633792 | tf_op jit(solution)/shard_map/convert_element_type | solution.py:955
  275.8 1.1 convert_element_type.40
  276.9 1.1 convert_element_type.41
  278.0 0.9 convert_bitcast_fusion
  278.9 0.7 convert_element_type.39
  (14 shorter events, 0.2 us)
Async XLA Ops:
  271.5 4.2 %copy-start.1 = (bf16[2,256,512]{2,1,0:T(8,128)(2,1)S(1)}, bf16[2,256,512]{2,1,0:T(8,128)(2,1)}, u32[]{:S(2)}) copy-start(bf16[2,256,512]{2,1,0:T(8,128)(2,1)} %get-tuple-element.27) | copy-start | bytes 1572868
  271.5 5.3 %copy-start = (bf16[2,256,512]{2,1,0:T(8,128)(2,1)S(1)}, bf16[2,256,512]{2,1,0:T(8,128)(2,1)}, u32[]{:S(2)}) copy-start(bf16[2,256,512]{2,1,0:T(8,128)(2,1)} %get-tuple-element.28) | copy-start | bytes 1572868
  275.8 2.2 copy-start.2
  275.8 3.2 %copy-start.3 = (bf16[2,256,128]{2,1,0:T(8,128)(2,1)S(1)}, bf16[2,256,128]{2,1,0:T(8,128)(2,1)}, u32[]{:S(2)}) copy-start(bf16[2,256,128]{2,1,0:T(8,128)(2,1)} %get-tuple-element.26) | copy-start | bytes 393220
